TPU v7x, 256 devices: a whole 4x4x8 slice. The times are simulated.
256 devices in a mesh: rep: 16 (over x, y_hi, core), shard: 16 (over z, y_lo).
Axes of the slice: x: 4, y: 4 (y_hi: 2, y_lo: 2; y = y_hi * 2 + y_lo), z: 8, core: 2. Of those that a mesh axis runs over, the one named last changes fastest.
Arguments:
- activations: bfloat16 [6, 32768, 2048], P(None, ('rep', 'shard')), may hold values from -50 to 50
- cotangents: bfloat16 [6, 32768, 512], P(None, ('rep', 'shard')), may hold values from -120 to 120
- momentum: float32 [12, 256, 2048], P(None, None, 'shard'), may hold values from -6 to 6
- owners: int32 [12], replicated, may hold values from 0 to 15, as said below
- bucket_starts: int32 [2], replicated, may hold values from 1 to 11, as said below
Outputs:
- momentum_out: float32 [12, 256, 2048], P(None, None, 'shard')
- update: float32 [12, 256, 2048], P(None, None, 'shard')
- owned: bfloat16 [32, 256, 2048], P('shard')
Inputs may be any that keep to these rules, and one draw needn't show every extreme that they name: `owners`: no owner is named more than 2 times, and some owner exactly 2 times. `bucket_starts`: strictly increasing.
All inputs are finite; a program needn't handle non-finite values.
Results may differ from a plain program's by a relative error of at most 0.033.
Values may be sent and summed in bfloat16 or wider, within the bound.
A program may use at most 128 MiB of HBM per device.

v0:
```python
import math

import jax
import jax.numpy as jnp
from jax import lax
from jax.sharding import Mesh
from jax.sharding import PartitionSpec as P

D = 2048
KV = 256
ITERS = 5
MATS = 12
SHARD = ("shard_0", "shard_1")
REP = ("rep_0", "rep_1", "rep_2")
REP_SHARD = ("rep_0", "rep_1", "rep_2", "shard_0", "shard_1")


coef_a = 3.4445
coef_b = -4.775
coef_c = 2.0315
momentum_rate = 0.95
clip_level = 0.5
epsilon = 1e-06


def scatter_axes(value, axes, dim):
    if not axes:
        return value
    nearer = lax.psum_scatter(value, axes[0], scatter_dimension=dim, tiled=True)
    return scatter_axes(nearer, axes[1:], dim)


def in_blocks(value, dim, devices):
    lengths = value.shape
    tiles = value.reshape(*lengths[:dim], devices, lengths[dim] // devices, *lengths[dim + 1 :])
    return jnp.moveaxis(tiles, dim, 0)


def sent_and_summed(value, axis, dim):
    tiles = in_blocks(value, dim, lax.axis_size(axis))
    arrived = lax.all_to_all(tiles, axis, split_axis=0, concat_axis=0, tiled=True)
    return arrived.astype(jnp.float32).sum(axis=0)


def summed_rows(value, axes, dim):
    far, near = axes
    own = sent_and_summed(in_blocks(value, dim, lax.axis_size(far)), near, dim + 1)
    return jnp.sum(
        lax.all_to_all(own.astype(jnp.bfloat16), far, 0, 0, tiled=True).astype(jnp.float32), axis=0
    )


def rows_for(lines, devices):
    spare = -len(lines) % devices
    return jnp.pad(lines, [(0, spare)] + [(0, 0)] * (lines.ndim - 1))


def from_everyone(value, axis):
    copies = jnp.broadcast_to(value, (lax.axis_size(axis), *value.shape))
    return lax.all_to_all(copies, axis, split_axis=0, concat_axis=0, tiled=True)


def in_order(tiles, dim):
    lengths = list(tiles.shape[1:])
    lengths[dim] *= tiles.shape[0]
    return jnp.moveaxis(tiles, 0, dim).reshape(lengths)


def gather_axes(value, axes, dim):
    far, near = axes
    tiles = from_everyone(from_everyone(value, far), near)
    return in_order(tiles.swapaxes(0, 1).reshape(-1, *value.shape), dim)


def sum_by_parts(value, axes):
    lines = value.reshape(-1, value.shape[-1])
    own = summed_rows(rows_for(lines, lax.axis_size(axes[0]) * lax.axis_size(axes[1])), axes, 0)
    whole = gather_axes(own.astype(jnp.bfloat16), axes, 0)
    return whole[: len(lines)].reshape(value.shape).astype(jnp.float32)


def orthogonal_batch(matrices):
    values = matrices.astype(jnp.float32)
    frobenius = jnp.sqrt(jnp.sum(values * values, axis=(1, 2), keepdims=True))
    matrix = (values / (frobenius + epsilon)).astype(jnp.bfloat16)
    for iteration in range(ITERS):
        gram_matrix = jnp.einsum(
            "skd,sjd->skj", matrix, matrix, preferred_element_type=jnp.float32
        ).astype(jnp.bfloat16)
        square = jnp.einsum(
            "skj,sji->ski", gram_matrix, gram_matrix, preferred_element_type=jnp.float32
        )
        mixing = (coef_b * gram_matrix.astype(jnp.float32) + coef_c * square).astype(jnp.bfloat16)
        product = jnp.einsum("skj,sjd->skd", mixing, matrix, preferred_element_type=jnp.float32)
        matrix = (coef_a * matrix.astype(jnp.float32) + product).astype(jnp.bfloat16)
    return matrix


def clip_factors(square_sums, bucket_starts):
    indices = jnp.arange(MATS, dtype=jnp.int32)
    buckets = jnp.sum((indices[:, None] >= bucket_starts[None, :]).astype(jnp.int32), axis=1)
    together = (buckets[:, None] == buckets[None, :]).astype(jnp.float32)
    totals = jnp.sum(together * square_sums[None, :], axis=1)
    members = jnp.sum(together, axis=1)
    root_mean = jnp.sqrt(totals / (members * KV * D) + epsilon)
    return jnp.minimum(1.0, clip_level / root_mean)


def slot_numbers(owners):
    indices = jnp.arange(MATS, dtype=jnp.int32)
    earlier = (indices[None, :] < indices[:, None]) & (owners[None, :] == owners[:, None])
    return jnp.sum(earlier.astype(jnp.int32), axis=1)


def selector(owner_of, slot_of, shard_count, slot_count):
    holders = lax.broadcasted_iota(jnp.int32, (shard_count, slot_count, 1), 0)
    places = lax.broadcasted_iota(jnp.int32, (shard_count, slot_count, 1), 1)
    chosen = (holders == owner_of[None, None, :]) & (places == slot_of[None, None, :])
    return chosen.astype(jnp.bfloat16)


def pack_slots(shards, chooser):
    return jnp.einsum("psm,mkd->skpd", chooser, shards, preferred_element_type=jnp.float32).astype(
        jnp.bfloat16
    )


def unpack_slots(received, chooser):
    return jnp.einsum("psm,skpd->mkd", chooser, received, preferred_element_type=jnp.float32)


def per_device(activations, cotangents, momentum, owners, bucket_starts):
    shard_count = lax.axis_size(SHARD)
    replica_count = lax.axis_size(REP)
    layers, tok_rows, width = activations.shape
    token_total = tok_rows * shard_count * replica_count
    columns = width // shard_count
    slot_count = -(-MATS // shard_count) + 1
    update_scale = math.sqrt(max(KV, D))
    partial_terms = jnp.einsum(
        "ltk,ltd->lkd", cotangents, activations, preferred_element_type=jnp.float32
    ).reshape(MATS, KV, width)
    shard_part = scatter_axes(partial_terms.astype(jnp.bfloat16), SHARD, 2).astype(jnp.float32)
    summed = sum_by_parts(shard_part.astype(jnp.bfloat16), (("rep_0", "rep_1"), "rep_2"))
    gradient = summed / jnp.sqrt(jnp.float32(token_total))
    square_sums = lax.psum(jnp.sum(gradient * gradient, axis=(1, 2)), SHARD)
    factors = clip_factors(square_sums, bucket_starts)
    momentum_out = momentum_rate * momentum + factors[:, None, None] * gradient
    nesterov = (factors[:, None, None] * gradient + momentum_rate * momentum_out).astype(
        jnp.bfloat16
    )
    slot_of = slot_numbers(owners)
    chooser = selector(owners, slot_of, shard_count, slot_count)
    received = lax.all_to_all(
        pack_slots(nesterov, chooser), SHARD, split_axis=2, concat_axis=2, tiled=True
    )
    item_count = received.shape[0]
    result = orthogonal_batch(received.reshape(item_count, KV, width))
    scaled = (update_scale * result.astype(jnp.float32)).astype(jnp.bfloat16)
    returned_part = lax.all_to_all(
        result.reshape(item_count, KV, shard_count, columns),
        SHARD,
        split_axis=2,
        concat_axis=2,
        tiled=True,
    )
    update = update_scale * unpack_slots(returned_part, chooser)
    return (momentum_out, update, scaled)


def solution(mesh):
    torus = Mesh(
        mesh.devices.reshape(4, 2, 2, 8, 2), ("rep_0", "rep_1", "rep_2", "shard_0", "shard_1")
    )
    return jax.shard_map(
        per_device,
        mesh=torus,
        in_specs=(
            P(None, REP_SHARD, None),
            P(None, REP_SHARD, None),
            P(None, None, SHARD),
            P(),
            P(),
        ),
        out_specs=(P(None, None, SHARD), P(None, None, SHARD), P(SHARD, None, None)),
        check_vma=False,
    )
```

profile of v0, /device:TPU:1, one launch (start us, length us, event | category | flops | bytes accessed | tf_op | source)
XLA Modules:
  0.0 413.3 jit_solution(5095224355678173759)
XLA Ops:
  7.2 1.8 copy-done
  9.1 7.5 %convolution_convert_fusion = bf16[6,512,2048]{2,1,0:T(8,128)(2,1)} fusion(bf16[6,128,512]{2,1,0:T(8,128)(2,1)} %param.6, bf16[6,128,2048]{2,1,0:T(8,128)(2,1)S(1)} %copy-done), kind=kOutput, calls=%fused_computation | convolution fusion | flops 1616904192 | bytes 16515072 | tf_op jit(solution)/shard_map/ltk,ltd->lkd/dot_general | solution.py:140
  16.7 138.4 %reduce-scatter.5.cloned.1.call-done = bf16[12,256,256]{2,1,0:T(8,128)(2,1)} async-done(((bf16[12,256,2048]{2,1,0:T(8,128)(2,1)}), bf16[12,256,256]{2,1,0:T(8,128)(2,1)}) %reduce-scatter.5.cloned.1.call-update) | async-done | bytes 1572880 | tf_op jit(solution)/shard_map/reduce_scatter | solution.py:29
  155.1 3.5 copy.66
  158.6 1.8 copy.68
  160.4 29.9 %reduce-scatter.7.cloned.1.call-done = bf16[128,3072]{1,0:T(8,128)(2,1)} async-done(((bf16[256,3072]{1,0:T(8,128)(2,1)}), bf16[128,3072]{1,0:T(8,128)(2,1)}) %reduce-scatter.7.cloned.1.call-update) | async-done | bytes 786448
  190.3 1.6 reshape.51
  191.9 0.9 copy.67
  192.9 4.8 %all_to_all.30 = bf16[2,8,192,128]{3,2,1,0:T(8,128)(2,1)S(1)} all-to-all(bf16[2,8,192,128]{3,2,1,0:T(8,128)(2,1)S(1)} %bitcast.65), channel_id=1, replica_groups=mesh['rep_0'=4,'rep_1'=2,'rep_2'=2,'shard_0'=8,'shard_1'=2] {'rep_2'}, dimensions={0} | all-to-all | bytes 1572864 | tf_op jit(solution)/shard_map/all_to_all | solution.py:41
  197.8 0.3 reduce_sum.87
  198.1 14.7 %all_to_all.31 = bf16[8,192,128]{2,1,0:T(8,128)(2,1)S(1)} all-to-all(bf16[8,192,128]{2,1,0:T(8,128)(2,1)S(1)} %reduce_sum.87), channel_id=1, replica_groups=mesh['rep_0'=4,'rep_1'=2,'rep_2'=2,'shard_0'=8,'shard_1'=2] {'rep_0','re..., dimensions={0} | all-to-all | bytes 786432 | tf_op jit(solution)/shard_map/all_to_all | solution.py:49
  212.8 0.1 reduce_sum.88
  212.8 0.8 broadcast_in_dim.4
  213.6 3.6 all-to-all-start.2
  217.2 0.2 convert_reduce_fusion
  217.4 7.6 %all-to-all-done.2 = bf16[8,192,128]{2,1,0:T(8,128)(2,1)S(1)} async-done(((bf16[8,192,128]{2,1,0:T(8,128)(2,1)}), bf16[8,192,128]{2,1,0:T(8,128)(2,1)S(1)}, u32[]{:S(2)}, u32[]{:S(2)}) %all-to-all-start.2) | async-done | bytes 393248 | tf_op jit(solution)/shard_map/all_to_all | solution.py:60
  225.0 0.1 broadcast_in_dim.5
  225.1 7.3 %all_to_all.32 = bf16[2,8,192,128]{3,2,1,0:T(8,128)(2,1)S(1)} all-to-all(bf16[2,8,192,128]{3,2,1,0:T(8,128)(2,1)S(1)} %broadcast_in_dim.5), channel_id=1, replica_groups=mesh['rep_0'=4,'rep_1'=2,'rep_2'=2,'shard_0'=8,'shard_1'=2] {'rep_2'}, dimensions={0} | all-to-all | bytes 1572864 | tf_op jit(solution)/shard_map/all_to_all | solution.py:60
  232.4 0.6 multiply_reduce_fusion.1
  233.1 0.1 reduce_sum.92
  233.2 0.1 reduce_sum.93
  233.3 0.1 fusion.47
  233.4 26.4 %psum.7 = f32[12]{0:T(128)S(1)} all-reduce(f32[12]{0:T(128)S(1)} %reduce_sum.93), channel_id=1, replica_groups=mesh['rep_0'=4,'rep_1'=2,'rep_2'=2,'shard_0'=8,'shard_1'=2] {'shard_0','..., use_global_device_ids=true, to_apply=%region_7.8 | all-reduce | flops 12 | bytes 96 | tf_op jit(solution)/shard_map/psum | solution.py:146
  259.7 0.2 fusion.41
  259.9 0.2 copy_convert_fusion.1
  260.1 3.0 fusion.15
  263.1 0.9 convert_bitcast_fusion
  264.0 2.0 copy.54
  266.0 48.6 %all_to_all.33 = bf16[2,256,16,128]{3,0,1,2:T(2,128)(2,1)S(1)} all-to-all(bf16[2,256,16,128]{3,0,1,2:T(2,128)(2,1)S(1)} %copy.54), channel_id=1, replica_groups=mesh['rep_0'=4,'rep_1'=2,'rep_2'=2,'shard_0'=8,'shard_1'=2] {'shard_0','..., dimensions={2} | all-to-all | bytes 4194304 | tf_op jit(solution)/shard_map/all_to_all | solution.py:154
  314.6 3.1 copy_convert_fusion
  317.8 4.9 %reshape.45 = f32[2,256,2048]{2,1,0:T(8,128)} reshape(f32[2,256,16,128]{3,2,1,0:T(8,128)} %copy_convert_fusion) | data formatting | bytes 8388608 | tf_op jit(solution)/shard_map/convert_element_type | solution.py:83
  322.7 2.3 multiply_reduce_fusion
  325.0 2.7 divide_convert_fusion
  327.7 0.7 convolution_convert_fusion.5
  328.4 2.3 add_convert_fusion.4
  330.7 3.1 convolution_convert_fusion.4
  333.8 2.3 add_convert_fusion.3
  336.1 3.1 convolution_convert_fusion.3
  339.2 2.3 add_convert_fusion.2
  341.5 3.0 convolution_convert_fusion.2
  344.5 3.2 add_convert_fusion.1
  347.7 0.7 convolution_convert_fusion.1
  348.4 3.2 multiply_convert_fusion
  351.6 2.2 copy.69
  353.8 2.4 copy.56
  356.2 47.2 %all_to_all.34 = bf16[2,256,16,128]{3,0,1,2:T(2,128)(2,1)S(1)} all-to-all(bf16[2,256,16,128]{3,0,1,2:T(2,128)(2,1)S(1)} %copy.56), channel_id=1, replica_groups=mesh['rep_0'=4,'rep_1'=2,'rep_2'=2,'shard_0'=8,'shard_1'=2] {'shard_0','..., dimensions={2} | all-to-all | bytes 4194304 | tf_op jit(solution)/shard_map/all_to_all | solution.py:160
  403.4 1.4 bitcast_multiply_fusion
  404.8 1.6 copy.58
  (18 shorter events, 0.2 us)
Async XLA Ops:
  7.2 1.9 copy-start
  7.2 147.9 %reduce-scatter.5.cloned.1.call-start = ((), (), s32[]{:S(2)}) async-start(), calls=%async_computation.8 | async-start | bytes 14155776 | tf_op jit(solution)/shard_map/reduce_scatter | solution.py:29
  16.6 173.7 %reduce-scatter.7.cloned.1.call-start = ((), (), s32[]{:S(2)}) async-start(), calls=%async_computation.9 | async-start | bytes 2359296
  197.8 19.4 %copy-start.4 = (s32[12]{0:T(128)S(1)}, s32[12]{0:T(128)}, u32[]{:S(2)}) copy-start(s32[12]{0:T(128)} %param.8) | copy-start | bytes 148
  213.6 19.7 %copy-start.5 = (s32[2]{0:T(128)S(1)}, s32[2]{0:T(128)}, u32[]{:S(2)}) copy-start(s32[2]{0:T(128)} %param.9) | copy-start | bytes 28
  213.6 11.3 %all-to-all-start.2 = ((bf16[8,192,128]{2,1,0:T(8,128)(2,1)}), bf16[8,192,128]{2,1,0:T(8,128)(2,1)S(1)}, u32[]{:S(2)}, u32[]{:S(2)}) async-start(bf16[8,192,128]{2,1,0:T(8,128)(2,1)} %broadcast_in_dim.4), calls=%async_computation.3 | async-start | bytes 786432 | tf_op jit(solution)/shard_map/all_to_all | solution.py:60
  330.7 3.1 copy-start.2
  336.1 3.1 copy-start.3
  403.4 3.0 copy-start.1
Sparse Core Ops, SparseCore 0:
  16.7 138.2 reduce-scatter.4
  160.6 29.7 reduce-scatter.6
where the time goes:
time: 420 us; the launch traced here: 413 us
  waiting for transfers between devices  176 us (42%)
  blocking collectives  149 us (35%)
  matrix products  33.6 us (8%)
  local copies, waits for them, and re-layouts  24 us (6%)
  between operations  14.2 us (3%)
  other arithmetic  12.8 us (3%)
    reduce_scatter x1, waiting for transfers between devices, scatter_axes(): nearer = lax.psum_scatter(value, axes[0], scatter_dimension=dim, tiled=True)  138 us
    all_to_all x1, blocking collectives, per_device(): lax.all_to_all(pack_slots(nesterov, chooser), SHARD, split_axis=2, concat...  48.6 us
    all_to_all x1, blocking collectives, per_device(): lax.all_to_all(result.reshape(item_count, KV, shard_count, columns), SHAR...  47.2 us
    unnamed x3, waiting for transfers between devices  29.9 us
    psum x1, blocking collectives, per_device(): square_sums = lax.psum(jnp.sum(gradient * gradient, axis=(1, 2)), SHARD)  26.4 us
    all_to_all x1, blocking collectives, summed_rows(): lax.all_to_all(own.astype(jnp.bfloat16), far, 0, 0, tiled=True)  14.7 us
    unnamed x18, local copies, waits for them, and re-layouts  13.6 us
    dot_general x5, matrix products, orthogonal_batch(): jnp.einsum('skj,sjd->skd', mixing, matrix, preferred_element_type=jnp.flo...  13.2 us
  transfers between devices with their start and end apart: 3, of which 3 were waited for; matrix products, arithmetic and copies ran while one was open for 0% of the time, Pallas kernels for 0%

commit v1 on v0

v1 whole, which is shorter than its diff:
```python
import functools
import math

import jax
import jax.numpy as jnp
from jax import lax
from jax.experimental import pallas as pl
from jax.experimental.pallas import tpu as pltpu
from jax.sharding import Mesh
from jax.sharding import PartitionSpec as P

D = 2048
KV = 256
ITERS = 5
MATS = 12
TOKENS = 32768
SHARD = ("shard_0", "shard_1")
REP_SHARD = ("rep_0", "rep_1", "rep_2", "shard_0", "shard_1")

coef_a = 3.4445
coef_b = -4.775
coef_c = 2.0315
momentum_rate = 0.95
clip_level = 0.5
epsilon = 1e-06

f32 = jnp.float32
bf16 = jnp.bfloat16
MESH = pl.DeviceIdType.MESH


def wrap(value, size):
    return lax.rem(value + 2 * size, size)


class Place:
    def __init__(self):
        self.x = lax.axis_index("rep_0")
        self.yh = lax.axis_index("rep_1")
        self.c = lax.axis_index("rep_2")
        self.z = lax.axis_index("shard_0")
        self.yl = lax.axis_index("shard_1")
        self.y = 2 * self.yh + self.yl
        self.block = 2 * self.x + self.yh
        self.column = 2 * self.z + self.yl

    def at(self, dx=0, dz=0):
        return (wrap(self.x + dx, 4), self.yh, self.c, wrap(self.z + dz, 8), self.yl)

    def at_y(self, dy):
        y = wrap(self.y + dy, 4)
        return (self.x, lax.div(y, 2), self.c, self.z, lax.rem(y, 2))

    def partner(self):
        return (self.x, self.yh, 1 - self.c, self.z, self.yl)

    def replicas(self):
        for dx in range(4):
            for dyh in range(2):
                if dx or dyh:
                    yield (wrap(self.x + dx, 4), lax.rem(self.yh + dyh, 2), self.c, self.z, self.yl)

    def columns(self):
        for dz in range(8):
            for dyl in range(2):
                if dz or dyl:
                    z, yl = wrap(self.z + dz, 8), lax.rem(self.yl + dyl, 2)
                    yield (self.x, self.yh, self.c, z, yl), 2 * z + yl


class Wire:
    def __init__(self, send_sems, recv_sems):
        self.send_sems, self.recv_sems = send_sems, recv_sems
        self.started = []

    def send(self, source, target, device):
        k = len(self.started)
        copy = pltpu.make_async_remote_copy(
            src_ref=source,
            dst_ref=target,
            send_sem=self.send_sems.at[k],
            recv_sem=self.recv_sems.at[k],
            device_id=device,
            device_id_type=MESH,
        )
        copy.start()
        self.started.append(copy)
        return copy

    def finish(self):
        for copy in self.started:
            copy.wait_send()


def greet(devices):
    barrier = pltpu.get_barrier_semaphore()
    devices = list(devices)
    for device in devices:
        pl.semaphore_signal(barrier, inc=1, device_id=device, device_id_type=MESH)
    pl.semaphore_wait(barrier, len(devices))


def rows_at(start, size):
    return pl.ds(pl.multiple_of(start, size), size)


Z_STEPS = {(0, 1): 4, (1, -1): 4, (1, 1): 3, (0, -1): 3}
Z_BASE = {(0, 1): 0, (1, -1): 4, (1, 1): 8, (0, -1): 11}
PAIR_BASE = {(0, 1): 0, (1, -1): 2, (1, 1): 4, (0, -1): 5}
PAIR_STEPS = {(0, 1): 2, (1, -1): 2, (1, 1): 1, (0, -1): 1}
REDUCE_SENDS = 6 + 14 + 6 + 6 + 9 + 17 + 7 + 7 + 15 + 2


def reduce_kernel(
    act, cot, g_out, sq_out,
    actv, cotv, cott, zs, zr, xs, xr, ys, yr,
    z2s, z2r, z3s, z3r, x2s, x2r, x3s, x3r, y2s, y2r, y3s, y3r,
    gb, sqs, sq2, sqb, local_sems, send_sems, recv_sems,
):
    me = Place()
    x, y, yh, yl, z, c = me.x, me.y, me.yh, me.yl, me.z, me.c
    wire = Wire(send_sems, recv_sems)
    mine = rows_at(c * 128, 128)

    loads = []
    for j in range(3):
        pair = (
            pltpu.make_async_copy(cot.at[3 * c + j], cotv.at[j, mine], local_sems.at[2 * j]),
            pltpu.make_async_copy(act.at[3 * c + j], actv.at[j, mine], local_sems.at[2 * j + 1]),
        )
        for copy in pair:
            copy.start()
        loads.append(pair)

    devices = [me.partner()]
    devices += [me.at(dx=d) for d in range(1, 4)]
    devices += [me.at_y(d) for d in range(1, 4)]
    devices += [(wrap(x + d, 4), 1 - yh, c, z, yl) for d in range(1, 4)]
    devices += [me.at(dz=d) for d in range(1, 8)]
    devices += [(x, yh, c, wrap(z + d, 8), 1 - yl) for d in range(1, 8)]
    greet(devices)

    swaps = []
    for j in range(3):
        swaps.append(
            (
                wire.send(cot.at[3 * (1 - c) + j], cotv.at[j, mine], me.partner()),
                wire.send(act.at[3 * (1 - c) + j], actv.at[j, mine], me.partner()),
            )
        )

    def prepare(j, inner_is_x):
        loads[j][0].wait()
        swaps[j][0].wait_recv()
        turned = cotv[j].T
        for bx in range(4):
            for by in range(2):
                for kv in range(2):
                    source = kv * 256 + (bx * 2 + by) * 32
                    target = (by * 256 + bx * 64 if inner_is_x else bx * 128 + by * 64) + kv * 32
                    cott[j, target : target + 32, :] = turned[source : source + 32, :]
        loads[j][1].wait()
        swaps[j][1].wait_recv()

    sent = {}

    def z_part(dest, half):
        columns = rows_at(dest * 256 + half * 128, 128)
        return jnp.dot(cott[0], actv[0, :, columns], preferred_element_type=f32)

    def z_send(half, d, n, k):
        part = z_part(wrap(z + d * (n + 1 - k), 8), half)
        slot = Z_BASE[half, d] + k - 1
        if k > 1:
            sent["z", half, d, k - 1].wait_recv()
            part += zr[slot - 1].astype(f32)
        zs[slot] = part.astype(bf16)
        sent["z", half, d, k] = wire.send(zs.at[slot], zr.at[slot], me.at(dz=d))

    def x_part(dest, half, i):
        columns = rows_at((4 * half + i) * 256, 256)
        return jnp.dot(cott[1, rows_at(dest * 128, 128), :], actv[1, :, columns], preferred_element_type=f32)

    def x_send(half, d, k):
        dest = wrap(x + d * (PAIR_STEPS[half, d] + 1 - k), 4)
        slot = PAIR_BASE[half, d] + k - 1
        if k > 1:
            sent["x", half, d, k - 1].wait_recv()

        def step(i, carry):
            part = x_part(dest, half, i)
            for t in range(2):
                value = part[:, t * 128 : (t + 1) * 128]
                if k > 1:
                    value += xr[slot - 1, 2 * i + t].astype(f32)
                xs[slot, 2 * i + t] = value.astype(bf16)
            return carry

        lax.fori_loop(0, 4, step, 0)
        sent["x", half, d, k] = wire.send(xs.at[slot], xr.at[slot], me.at(dx=d))

    def y_part(dest, half, i):
        columns = rows_at(((4 * half + i) * 2 + lax.rem(dest, 2)) * 128, 128)
        rows = rows_at(lax.div(dest, 2) * 256, 256)
        return jnp.dot(cott[2, rows, :], actv[2, :, columns], preferred_element_type=f32)

    def y_send(half, d, k):
        dest = wrap(y + d * (PAIR_STEPS[half, d] + 1 - k), 4)
        slot = PAIR_BASE[half, d] + k - 1
        if k > 1:
            sent["y", half, d, k - 1].wait_recv()

        def step(i, carry):
            value = y_part(dest, half, i)
            if k > 1:
                value += yr[slot - 1, i].astype(f32)
            ys[slot, i] = value.astype(bf16)
            return carry

        lax.fori_loop(0, 4, step, 0)
        sent["y", half, d, k] = wire.send(ys.at[slot], yr.at[slot], me.at_y(d))

    def z_round(k):
        for (half, d), n in Z_STEPS.items():
            if k <= n:
                z_send(half, d, n, k)

    prepare(0, False)
    z_round(1)
    prepare(1, False)
    x_send(0, 1, 1)
    x_send(1, -1, 1)
    prepare(2, True)
    y_send(0, 1, 1)
    y_send(1, -1, 1)
    x_send(1, 1, 1)
    x_send(0, -1, 1)
    y_send(1, 1, 1)
    y_send(0, -1, 1)
    z_round(2)
    x_send(0, 1, 2)
    x_send(1, -1, 2)
    y_send(0, 1, 2)
    y_send(1, -1, 2)
    z_round(3)
    z_round(4)

    for half in range(2):
        sent["x", half, 1, PAIR_STEPS[half, 1]].wait_recv()
        sent["x", half, -1, PAIR_STEPS[half, -1]].wait_recv()
        up = PAIR_BASE[half, 1] + PAIR_STEPS[half, 1] - 1
        down = PAIR_BASE[half, -1] + PAIR_STEPS[half, -1] - 1

        def x_last(i, carry, half=half, up=up, down=down):
            part = x_part(x, half, i)
            for t in range(2):
                value = part[:, t * 128 : (t + 1) * 128]
                value += xr[up, 2 * i + t].astype(f32) + xr[down, 2 * i + t].astype(f32)
                x2s[t, 4 * half + i] = value.astype(bf16)
            return carry

        lax.fori_loop(0, 4, x_last, 0)
    for d in (1, 3, 2):
        to = wrap(y + d, 4)
        sent["x2", d] = wire.send(
            x2s.at[lax.rem(to, 2), :, rows_at(lax.div(to, 2) * 64, 64), :], x2r.at[d - 1], me.at_y(d)
        )

    for half in range(2):
        sent["y", half, 1, PAIR_STEPS[half, 1]].wait_recv()
        sent["y", half, -1, PAIR_STEPS[half, -1]].wait_recv()
        up = PAIR_BASE[half, 1] + PAIR_STEPS[half, 1] - 1
        down = PAIR_BASE[half, -1] + PAIR_STEPS[half, -1] - 1

        def y_last(i, carry, half=half, up=up, down=down):
            value = y_part(y, half, i) + yr[up, i].astype(f32) + yr[down, i].astype(f32)
            y2s[4 * half + i] = value.astype(bf16)
            return carry

        lax.fori_loop(0, 4, y_last, 0)
    for d in (1, 3, 2):
        to = wrap(x + d, 4)
        sent["y2", d] = wire.send(y2s.at[:, rows_at(to * 64, 64), :], y2r.at[d - 1], me.at(dx=d))

    for half in range(2):
        last = []
        for d in (1, -1):
            n = Z_STEPS[half, d]
            sent["z", half, d, n].wait_recv()
            last.append(Z_BASE[half, d] + n - 1)
        value = z_part(z, half) + zr[last[0]].astype(f32) + zr[last[1]].astype(f32)
        z2s[half] = value.astype(bf16)
    for d in (1, 3, 2):
        to = wrap(x + d, 4)
        sent["z2", d] = wire.send(z2s.at[:, rows_at(to * 128, 128), :], z2r.at[d - 1], me.at(dx=d))

    for d in range(1, 4):
        sent["x2", d].wait_recv()

    def x_third(i, carry):
        value = x2s[yl, i, rows_at(yh * 64, 64), :].astype(f32)
        for d in range(3):
            value += x2r[d, i].astype(f32)
        x3s[i] = value.astype(bf16)
        return carry

    lax.fori_loop(0, 8, x_third, 0)
    for d in (4, 3, 5, 2, 6, 1, 7):
        sent["x3", d] = wire.send(x3s.at[wrap(z + d, 8)], x3r.at[d - 1], me.at(dz=d))

    for d in range(1, 4):
        sent["y2", d].wait_recv()

    def y_third(i, carry):
        value = y2s[i, rows_at(x * 64, 64), :].astype(f32)
        for d in range(3):
            value += y2r[d, i].astype(f32)
        y3s[i] = value.astype(bf16)
        return carry

    lax.fori_loop(0, 8, y_third, 0)
    for d in (4, 3, 5, 2, 6, 1, 7):
        sent["y3", d] = wire.send(y3s.at[wrap(z + d, 8)], y3r.at[d - 1], me.at(dz=d))

    for d in range(1, 4):
        sent["z2", d].wait_recv()
    for t in range(2):
        value = z2s[t, rows_at(x * 128, 128), :].astype(f32)
        for d in range(3):
            value += z2r[d, t].astype(f32)
        z3s[t] = value.astype(bf16)
    for d in (2, 1, 3):
        to = wrap(y + d, 4)
        sent["z3", d] = wire.send(
            z3s.at[lax.rem(to, 2), rows_at(lax.div(to, 2) * 64, 64), :], z3r.at[d - 1], me.at_y(d)
        )

    rows = rows_at(me.block * 32, 32)
    inverse = 1.0 / math.sqrt(TOKENS)
    sqs[me.block] = jnp.zeros((8, 128), f32)

    def piece(j, value):
        value = value * inverse
        for kv in range(2):
            block = value[kv * 32 : (kv + 1) * 32]
            gb[6 * c + 2 * j + kv, rows, :] = block.astype(bf16)
            total = jnp.sum(block * block, axis=(0, 1), keepdims=True)
            sqs[me.block, 2 * j + kv : 2 * j + kv + 1, :] = jnp.broadcast_to(total, (1, 128))

    for d in range(1, 8):
        sent["x3", d].wait_recv()
    value = x3s[z].astype(f32)
    for d in range(7):
        value += x3r[d].astype(f32)
    piece(1, value)
    for d in range(1, 8):
        sent["y3", d].wait_recv()
    value = y3s[z].astype(f32)
    for d in range(7):
        value += y3r[d].astype(f32)
    piece(2, value)
    for d in range(1, 4):
        sent["z3", d].wait_recv()
    value = z3s[yl, rows_at(yh * 64, 64), :].astype(f32)
    for d in range(3):
        value += z3r[d].astype(f32)
    piece(0, value)

    own = pl.ds(6 * c, 6)
    squares = [wire.send(sqs.at[me.block], sqs.at[me.block], device) for device in me.replicas()]
    pieces = [wire.send(gb.at[own, rows, :], gb.at[own, rows, :], device) for device in me.replicas()]
    for copy in squares:
        copy.wait_recv()
    sq2[me.column] = sum((sqs[i] for i in range(1, 8)), sqs[0])
    squares = [wire.send(sq2.at[me.column], sq2.at[me.column], device) for device, _ in me.columns()]
    for copy in pieces:
        copy.wait_recv()
    over = wire.send(gb.at[own], gb.at[own], me.partner())
    for copy in squares:
        copy.wait_recv()
    sqb[c] = sum((sq2[i] for i in range(1, 16)), sq2[0])
    other = wire.send(sqb.at[c], sqb.at[c], me.partner())
    over.wait_recv()
    store = pltpu.make_async_copy(gb, g_out, local_sems.at[6])
    store.start()
    other.wait_recv()
    sq_out[...] = sqb[...]
    store.wait()
    wire.finish()


def reduced(act, cot):
    vm = pltpu.VMEM
    return pl.pallas_call(
        reduce_kernel,
        out_shape=(
            jax.ShapeDtypeStruct((MATS, KV, 128), bf16),
            jax.ShapeDtypeStruct((2, 8, 128), f32),
        ),
        in_specs=[pl.BlockSpec(memory_space=pl.ANY)] * 2,
        out_specs=(pl.BlockSpec(memory_space=pl.ANY), pl.BlockSpec(memory_space=pltpu.VMEM)),
        scratch_shapes=[
            vm((3, 256, D), bf16), vm((3, 256, 512), bf16), vm((3, 512, 256), bf16),
            vm((14, 512, 128), bf16), vm((14, 512, 128), bf16),
            vm((6, 8, 128, 128), bf16), vm((6, 8, 128, 128), bf16),
            vm((6, 4, 256, 128), bf16), vm((6, 4, 256, 128), bf16),
            vm((2, 512, 128), bf16), vm((3, 2, 128, 128), bf16), vm((2, 128, 128), bf16), vm((3, 64, 128), bf16),
            vm((2, 8, 128, 128), bf16), vm((3, 8, 64, 128), bf16), vm((8, 64, 128), bf16), vm((7, 64, 128), bf16),
            vm((8, 256, 128), bf16), vm((3, 8, 64, 128), bf16), vm((8, 64, 128), bf16), vm((7, 64, 128), bf16),
            vm((MATS, KV, 128), bf16), vm((8, 8, 128), f32), vm((16, 8, 128), f32), vm((2, 8, 128), f32),
            pltpu.SemaphoreType.DMA((7,)),
            pltpu.SemaphoreType.DMA((REDUCE_SENDS,)),
            pltpu.SemaphoreType.DMA((REDUCE_SENDS,)),
        ],
        compiler_params=pltpu.CompilerParams(
            collective_id=0, has_side_effects=True, vmem_limit_bytes=60 * 1024 * 1024
        ),
        name="reduce",
    )(act, cot)


def orthogonalize(xin, xw):
    def squares(i, total):
        value = xin[rows_at(i * 16, 16), :].astype(f32)
        return total + value * value

    total = lax.fori_loop(0, 16, squares, jnp.zeros((16, D), f32))
    norm = jnp.sqrt(jnp.sum(total, axis=(0, 1), keepdims=True))
    scale = 1.0 / (norm + epsilon)

    def start(i, carry):
        xw[rows_at(i * 16, 16), :] = (xin[rows_at(i * 16, 16), :].astype(f32) * scale).astype(bf16)
        return carry

    lax.fori_loop(0, 16, start, 0)

    def iteration(i, carry):
        gram = lax.dot_general(xw[...], xw[...], (((1,), (1,)), ((), ())), preferred_element_type=f32).astype(bf16)
        square = jnp.dot(gram, gram, preferred_element_type=f32)
        mixing = (coef_b * gram.astype(f32) + coef_c * square).astype(bf16)
        for k in range(4):
            cols = slice(k * 512, (k + 1) * 512)
            old = xw[:, cols]
            product = jnp.dot(mixing, old, preferred_element_type=f32)
            xw[:, cols] = (coef_a * old.astype(f32) + product).astype(bf16)
        return carry

    lax.fori_loop(0, ITERS, iteration, 0)


OWNER_SENDS = 15 + 7 + 1 + 15 + 1 + 7 + 1


def owner_kernel(
    owners, u, upd_out, o_out, ub, xin, xw, rb, ob, us, local_sems, send_sems, recv_sems
):
    me = Place()
    c = me.c
    wire = Wire(send_sems, recv_sems)
    load = pltpu.make_async_copy(u, ub, local_sems.at[0])
    load.start()
    devices = [me.partner()] + list(me.replicas()) + [device for device, _ in me.columns()]
    greet(devices)
    load.wait()
    rows = rows_at(me.block * 32, 32)

    def choose(p, carry):
        found, seen = jnp.int32(0), jnp.int32(0)
        filled = jnp.int32(0)
        for m in range(MATS):
            held = (owners[m] == p).astype(jnp.int32)
            take = held * (seen == c).astype(jnp.int32)
            found = found + take * m
            filled = filled + take
            seen = seen + held
        block = ub[found, rows, :].astype(f32) * filled.astype(f32)
        us[p] = block.astype(bf16)
        return carry

    lax.fori_loop(0, 16, choose, 0)
    here = rows_at(me.column * 128, 128)
    copies = [wire.send(us.at[p], xin.at[rows, here], device) for device, p in me.columns()]
    xin[rows, here] = us[me.column]
    for copy in copies:
        copy.wait_recv()
    copies = [wire.send(xin.at[rows, :], xin.at[rows, :], device) for device in me.replicas()]
    for copy in copies:
        copy.wait_recv()

    orthogonalize(xin, xw)

    copies = [
        wire.send(xw.at[rows, rows_at(p * 128, 128)], rb.at[c, me.column], device)
        for device, p in me.columns()
    ]
    rb[c, me.column] = xw[rows, here]
    whole = wire.send(xw, o_out.at[c], me.partner())
    store = pltpu.make_async_copy(xw, o_out.at[c], local_sems.at[1])
    store.start()
    for copy in copies:
        copy.wait_recv()
    over = wire.send(rb.at[c], rb.at[c], me.partner())
    over.wait_recv()
    for k in range(6):
        m = 6 * c + k
        owner = owners[m]
        slot = jnp.int32(0)
        for j in range(MATS):
            slot = slot + (owners[j] == owner).astype(jnp.int32) * (j < m).astype(jnp.int32)
        ob[m, rows, :] = rb[jnp.minimum(slot, 1), owner]
    own = pl.ds(6 * c, 6)
    copies = [wire.send(ob.at[own, rows, :], ob.at[own, rows, :], device) for device in me.replicas()]
    for copy in copies:
        copy.wait_recv()
    over = wire.send(ob.at[own], ob.at[own], me.partner())
    over.wait_recv()
    out = pltpu.make_async_copy(ob, upd_out, local_sems.at[2])
    out.start()
    whole.wait_recv()
    store.wait()
    out.wait()
    wire.finish()


def orthogonal_pieces(u, owners):
    vm = pltpu.VMEM
    return pl.pallas_call(
        owner_kernel,
        out_shape=(
            jax.ShapeDtypeStruct((MATS, KV, 128), bf16),
            jax.ShapeDtypeStruct((2, KV, D), bf16),
        ),
        in_specs=[pl.BlockSpec(memory_space=pltpu.SMEM), pl.BlockSpec(memory_space=pl.ANY)],
        out_specs=(pl.BlockSpec(memory_space=pl.ANY), pl.BlockSpec(memory_space=pl.ANY)),
        scratch_shapes=[
            vm((MATS, KV, 128), bf16), vm((KV, D), bf16), vm((KV, D), bf16), vm((2, 16, 32, 128), bf16),
            vm((MATS, KV, 128), bf16), vm((16, 32, 128), bf16),
            pltpu.SemaphoreType.DMA((3,)),
            pltpu.SemaphoreType.DMA((OWNER_SENDS,)),
            pltpu.SemaphoreType.DMA((OWNER_SENDS,)),
        ],
        compiler_params=pltpu.CompilerParams(
            collective_id=1, has_side_effects=True, vmem_limit_bytes=60 * 1024 * 1024
        ),
        name="owner",
    )(owners, u)


def clip_factors(square_sums, bucket_starts):
    indices = jnp.arange(MATS, dtype=jnp.int32)
    buckets = jnp.sum((indices[:, None] >= bucket_starts[None, :]).astype(jnp.int32), axis=1)
    together = (buckets[:, None] == buckets[None, :]).astype(f32)
    totals = jnp.sum(together * square_sums[None, :], axis=1)
    members = jnp.sum(together, axis=1)
    root_mean = jnp.sqrt(totals / (members * KV * D) + epsilon)
    return jnp.minimum(1.0, clip_level / root_mean)


def per_device(activations, cotangents, momentum, owners, bucket_starts):
    update_scale = math.sqrt(max(KV, D))
    gradient, squares = reduced(activations, cotangents)
    gradient = gradient.astype(f32)
    factors = clip_factors(squares[:, :6, 0].reshape(MATS), bucket_starts)
    momentum_out = momentum_rate * momentum + factors[:, None, None] * gradient
    nesterov = (factors[:, None, None] * gradient + momentum_rate * momentum_out).astype(bf16)
    returned, whole = orthogonal_pieces(nesterov, owners)
    update = update_scale * returned.astype(f32)
    owned = (update_scale * whole.astype(f32)).astype(bf16)
    return (momentum_out, update, owned)


def solution(mesh):
    torus = Mesh(
        mesh.devices.reshape(4, 2, 2, 8, 2), ("rep_0", "rep_1", "rep_2", "shard_0", "shard_1")
    )
    return jax.shard_map(
        per_device,
        mesh=torus,
        in_specs=(
            P(None, REP_SHARD, None),
            P(None, REP_SHARD, None),
            P(None, None, SHARD),
            P(),
            P(),
        ),
        out_specs=(P(None, None, SHARD), P(None, None, SHARD), P(SHARD, None, None)),
        check_vma=False,
    )
```

time: 420 us -> 130 us (0.31); the launches traced: 413 us -> 129 us
  waiting for transfers between devices: 176 us -> 0 us
  blocking collectives: 149 us -> 0 us
  Pallas kernels: 0 us -> 120 us
  matrix products: 33.6 us -> 0 us
  local copies, waits for them, and re-layouts: 24 us -> 0.88 us
  between operations: 14.2 us -> 0.68 us
  other arithmetic: 12.8 us -> 8.07 us
    reduce_scatter x1 -> x0, waiting for transfers between devices: 138 us -> none  [scatter_axes(): nearer = lax.psum_scatter(value, axes[0], scatter_dimension=dim, tiled=True)]
    all_to_all x5 -> x0, blocking collectives: 123 us -> none  [the longest x1 48.6 us: per_device(): lax.all_to_all(pack_slots(nesterov, chooser), SHARD, split_axis=2, concat...]
    pallas_call x0 -> x2, Pallas kernels: none -> 120 us  [the longest x1 65.5 us: reduced(): pl.pallas_call(reduce_kernel, out_shape=(jax.ShapeDtypeStruct((MATS, KV,...]
    dot_general x13 -> x0, matrix products: 33.6 us -> none  [the longest x5 13.2 us: orthogonal_batch(): jnp.einsum('skj,sjd->skd', mixing, matrix, preferred_element_type=jnp.flo...]
    unnamed x3 -> x0, waiting for transfers between devices: 29.9 us -> none
    psum x1 -> x0, blocking collectives: 26.4 us -> none  [per_device(): square_sums = lax.psum(jnp.sum(gradient * gradient, axis=(1, 2)), SHARD)]
    unnamed x18 -> x6, local copies, waits for them, and re-layouts: 13.6 us -> 0.01 us
    all_to_all x1 -> x0, waiting for transfers between devices: 7.56 us -> none  [from_everyone(): return lax.all_to_all(copies, axis, split_axis=0, concat_axis=0, tiled=True)]
  transfers between devices with their start and end apart: 3 -> 0, of which waited for: 3 -> 0; matrix products, arithmetic and copies ran while one was open for 0% -> 0% of each run, Pallas kernels for 0% -> 0%
where the time goes in v1:
time: 130 us; the launch traced here: 129 us
  Pallas kernels  120 us (92%)
  other arithmetic  8.07 us (6%)
    pallas_call x1, Pallas kernels, reduced(): pl.pallas_call(reduce_kernel, out_shape=(jax.ShapeDtypeStruct((MATS, KV,...  65.5 us
    pallas_call x1, Pallas kernels, orthogonal_pieces(): pl.pallas_call(owner_kernel, out_shape=(jax.ShapeDtypeStruct((MATS, KV, 1...  54.3 us
    convert_element_type x1, other arithmetic, per_device(): owned = (update_scale * whole.astype(f32)).astype(bf16)  3.52 us
    convert_element_type x1, other arithmetic, per_device(): (factors[:, None, None] * gradient + momentum_rate * momentum_out).astype...  2.97 us

profile of v1, /device:TPU:1, one launch (start us, length us, event | category | flops | bytes accessed | tf_op | source)
XLA Modules:
  0.0 129.4 jit_solution(12357422631267761297)
XLA Ops:
  0.6 0.0 copy-start.2
  0.6 0.0 copy-start
  0.7 65.5 %reduce.3 = (bf16[12,256,128]{2,1,0:T(8,128)(2,1)}, f32[2,8,128]{2,1,0:T(8,128)}) custom-call(bf16[6,128,2048]{2,1,0:T(8,128)(2,1)} %act.1, bf16[6,128,512]{2,1,0:T(8,128)(2,1)} %cot.1), custom_call_target="tpu_custom_call" | custom-call | tf_op jit(solution)/shard_map/reduce/pallas_call | solution.py:394
  66.2 0.8 slice_reduce_fusion
  66.9 0.1 mul.51
  67.0 0.0 copy-done.2
  67.0 0.1 fusion.3
  67.1 0.2 fusion.2
  67.3 0.0 copy-done
  67.3 3.0 %add_convert_fusion = (bf16[12,256,128]{2,1,0:T(8,128)(2,1)}, f32[12,256,128]{2,1,0:T(8,128)}) fusion(bf16[12,256,128]{2,1,0:T(8,128)(2,1)} %get-tuple-element.8, f32[12]{0:T(128)S(1)} %multiply_minimum_fusion, f32[12,256,128]{2,1,0:T(8,128)S(1)} %copy-done), kind=kLoop, calls=%fused_computation.2 | loop fusion | flops 2752512 | bytes 4718640 | tf_op jit(solution)/shard_map/convert_element_type | solution.py:565
  70.3 54.3 %owner.1 = (bf16[12,256,128]{2,1,0:T(8,128)(2,1)}, bf16[2,256,2048]{2,1,0:T(8,128)(2,1)}) custom-call(s32[12]{0:T(128)} %owners.1, bf16[12,256,128]{2,1,0:T(8,128)(2,1)} %get-tuple-element.13.u), custom_call_target="tpu_custom_call" | custom-call | tf_op jit(solution)/shard_map/owner/pallas_call | solution.py:527
  124.6 0.0 copy-start.1
  124.6 3.5 %multiply_convert_fusion = bf16[2,256,2048]{2,1,0:T(8,128)(2,1)} fusion(bf16[2,256,2048]{2,1,0:T(8,128)(2,1)} %get-tuple-element.10), kind=kLoop, calls=%fused_computation | loop fusion | flops 3145728 | bytes 4194304 | tf_op jit(solution)/shard_map/convert_element_type | solution.py:568
  128.1 0.0 copy-done.1
  128.1 1.3 %convert_multiply_fusion = f32[12,256,128]{2,1,0:T(8,128)} fusion(bf16[12,256,128]{2,1,0:T(8,128)(2,1)S(1)} %copy-done.1), kind=kLoop, calls=%fused_computation.1 | loop fusion | flops 786432 | bytes 2359296 | tf_op jit(solution)/shard_map/mul | solution.py:567
  (1 shorter events, 0.0 us)
Async XLA Ops:
  0.6 66.4 %copy-start.2 = (s32[2]{0:T(128)S(1)}, s32[2]{0:T(128)}, u32[]{:S(2)}) copy-start(s32[2]{0:T(128)} %param.9) | copy-start | bytes 28
  0.6 66.7 %copy-start = (f32[12,256,128]{2,1,0:T(8,128)S(1)}, f32[12,256,128]{2,1,0:T(8,128)}, u32[]{:S(2)}) copy-start(f32[12,256,128]{2,1,0:T(8,128)} %param.7) | copy-start | bytes 4718596
  124.6 3.5 %copy-start.1 = (bf16[12,256,128]{2,1,0:T(8,128)(2,1)S(1)}, bf16[12,256,128]{2,1,0:T(8,128)(2,1)}, u32[]{:S(2)}) copy-start(bf16[12,256,128]{2,1,0:T(8,128)(2,1)} %get-tuple-element.9) | copy-start | bytes 2359300

commit v2 on v1

v2 whole, which is shorter than its diff:
```python
import functools
import math

import jax
import jax.numpy as jnp
from jax import lax
from jax.experimental import pallas as pl
from jax.experimental.pallas import tpu as pltpu
from jax.sharding import Mesh
from jax.sharding import PartitionSpec as P

D = 2048
KV = 256
ITERS = 5
MATS = 12
TOKENS = 32768
SHARD = ("shard_0", "shard_1")
REP_SHARD = ("rep_0", "rep_1", "rep_2", "shard_0", "shard_1")

coef_a = 3.4445
coef_b = -4.775
coef_c = 2.0315
momentum_rate = 0.95
clip_level = 0.5
epsilon = 1e-06

f32 = jnp.float32
bf16 = jnp.bfloat16
MESH = pl.DeviceIdType.MESH


def wrap(value, size):
    return lax.rem(value + 2 * size, size)


class Place:
    def __init__(self):
        self.x = lax.axis_index("rep_0")
        self.yh = lax.axis_index("rep_1")
        self.c = lax.axis_index("rep_2")
        self.z = lax.axis_index("shard_0")
        self.yl = lax.axis_index("shard_1")
        self.y = 2 * self.yh + self.yl
        self.block = 2 * self.x + self.yh
        self.column = 2 * self.z + self.yl

    def at(self, dx=0, dz=0):
        return (wrap(self.x + dx, 4), self.yh, self.c, wrap(self.z + dz, 8), self.yl)

    def at_y(self, dy):
        y = wrap(self.y + dy, 4)
        return (self.x, lax.div(y, 2), self.c, self.z, lax.rem(y, 2))

    def partner(self):
        return (self.x, self.yh, 1 - self.c, self.z, self.yl)

    def replicas(self):
        for dx in range(4):
            for dyh in range(2):
                if dx or dyh:
                    yield (wrap(self.x + dx, 4), lax.rem(self.yh + dyh, 2), self.c, self.z, self.yl)

    def columns_at(self, dz):
        for dyl in range(2):
            if dz or dyl:
                z, yl = wrap(self.z + dz, 8), lax.rem(self.yl + dyl, 2)
                yield (self.x, self.yh, self.c, z, yl), 2 * z + yl

    def columns(self):
        for dz in (4, 3, 5, 2, 6, 1, 7, 0):
            yield from self.columns_at(dz)


class Wire:
    def __init__(self, send_sems, recv_sems, device):
        self.send_sems, self.recv_sems, self.device = send_sems, recv_sems, device
        self.n_send = self.n_recv = 0
        self.leaving, self.kept, self.numbers = [], [], {}

    def copy(self, source, target, s, r, device):
        return pltpu.make_async_remote_copy(
            src_ref=source,
            dst_ref=target,
            send_sem=self.send_sems.at[s],
            recv_sem=self.recv_sems.at[r],
            device_id=device,
            device_id_type=MESH,
        )

    def outlet(self, whole):
        self.n_send += 1
        self.leaving.append((self.n_send - 1, whole))
        return self.n_send - 1

    def send(self, source, target, device, s=None):
        if s is None:
            s = self.outlet(source)
        r = self.n_recv
        self.n_recv += 1
        copy = self.copy(source, target, s, r, device)
        copy.start()
        return copy

    def opened(self, whole):
        s, r = self.outlet(whole), self.n_recv
        self.n_recv += 1
        copy = self.copy(whole, whole, s, r, self.device)
        self.kept.append(copy)
        self.numbers[id(copy)] = (s, r)
        return copy

    def join(self, group, copies):
        for source, target, device in copies:
            self.copy(source, target, *self.numbers[id(group)], device).start()

    def group(self, copies, whole):
        group = self.opened(whole)
        self.join(group, copies)
        return group

    def finish(self):
        assert (self.n_send, self.n_recv) == (OUTLETS, ARRIVALS), (self.n_send, self.n_recv)
        for s, whole in self.leaving:
            self.copy(whole, whole, s, 0, self.device).wait_send()


def signal_all(devices):
    barrier = pltpu.get_barrier_semaphore()
    for device in devices:
        pl.semaphore_signal(barrier, inc=1, device_id=device, device_id_type=MESH)


class Phases:
    def __init__(self):
        self.open = None

    def __call__(self, name):
        self.end()
        self.open = jax.named_scope(name)
        self.open.__enter__()

    def end(self):
        if self.open:
            self.open.__exit__(None, None, None)
        self.open = None


def rows_at(start, size):
    return pl.ds(pl.multiple_of(start, size), size)


Z_STEPS = {(0, 1): 4, (1, -1): 4, (1, 1): 3, (0, -1): 3}
Z_BASE = {(0, 1): 0, (1, -1): 4, (1, 1): 8, (0, -1): 11}
PAIR_BASE = {(0, 1): 0, (1, -1): 2, (1, 1): 4, (0, -1): 5}
PAIR_STEPS = {(0, 1): 2, (1, -1): 2, (1, 1): 1, (0, -1): 1}
OUTLETS, ARRIVALS = 24, 51


def step_kernel(
    owners_in, starts_in, act, cot, mom, g_out, f_out, upd_out, o_out,
    cin, cout, aout, actv, cott, zs, zr, xs, xr, ys, yr,
    z2s, z2r, z3s, z3r, x2s, x2r, x3s, x3r, y2s, y2r, y3s, y3r,
    gb, gp, sqs, sq2, mb, us, ms, fac, gq, mq, gin, xw, rb, ob, gram, owners, starts, table, local_sems, send_sems, recv_sems,
):
    me = Place()
    x, y, yh, yl, z, c = me.x, me.y, me.yh, me.yl, me.z, me.c
    wire = Wire(send_sems, recv_sems, me.partner())
    phase = Phases()
    mine = rows_at(c * 128, 128)

    load_cot = pltpu.make_async_copy(cot, cin, local_sems.at[0])
    load_cot.start()
    loads, loads_out = [], []
    for j in range(3):
        loads_out.append(pltpu.make_async_copy(act.at[3 * (1 - c) + j], aout.at[j], local_sems.at[1 + j]))
        loads.append(pltpu.make_async_copy(act.at[3 * c + j], actv.at[j, mine], local_sems.at[4 + j]))
        loads_out[j].start()
        loads[j].start()
    rows = rows_at(me.block * 32, 32)
    load_momentum = pltpu.make_async_copy(mom.at[:, rows, :], mb, local_sems.at[12])
    load_momentum.start()
    load_owners = pltpu.make_async_copy(owners_in, owners, local_sems.at[10])
    load_starts = pltpu.make_async_copy(starts_in, starts, local_sems.at[11])
    load_owners.start()
    load_starts.start()

    phase("r_greet")
    devices = [me.partner()]
    devices += [me.at(dx=d) for d in range(1, 4)]
    devices += [me.at_y(d) for d in range(1, 4)]
    devices += [(wrap(x + d, 4), 1 - yh, c, z, yl) for d in range(1, 4)]
    devices += [(dx, dy, 1 - c, dz, dl) for dx, dy, _, dz, dl in me.replicas()]
    devices += [me.at(dz=d) for d in range(1, 8)]
    devices += [(x, yh, c, wrap(z + d, 8), 1 - yl) for d in range(1, 8)]
    signal_all(devices)

    def turn(source, store, inner_is_x):
        turned = source.T
        for bx in range(4):
            for by in range(2):
                for kv in range(2):
                    at = kv * 256 + (bx * 2 + by) * 32
                    to = (by * 256 + bx * 64 if inner_is_x else bx * 128 + by * 64) + kv * 32
                    store(to, turned[at : at + 32, :])

    load_cot.wait()
    for j in range(3):

        def store_out(to, value, j=j):
            cout[j, to : to + 32, :] = value

        def store_own(to, value, j=j):
            cott[j, to : to + 32, mine] = value

        turn(cin[3 * (1 - c) + j], store_out, j == 2)
        turn(cin[3 * c + j], store_own, j == 2)

    phase("r_greetw")
    pl.semaphore_wait(pltpu.get_barrier_semaphore(), len(devices))
    phase("r_swap")
    out_cot, out_act = wire.outlet(cout), wire.outlet(aout)
    out_x, out_y, out_z = wire.outlet(xs), wire.outlet(ys), wire.outlet(zs)
    swaps = []
    for j in range(3):
        loads_out[j].wait()
        swaps.append(
            (
                wire.send(cout.at[j], cott.at[j, :, mine], me.partner(), out_cot),
                wire.send(aout.at[j], actv.at[j, mine], me.partner(), out_act),
            )
        )

    def prepare(j):
        loads[j].wait()
        swaps[j][0].wait_recv()
        swaps[j][1].wait_recv()

    sent = {}

    def z_part(dest, half):
        columns = rows_at(dest * 256 + half * 128, 128)
        return jnp.dot(cott[0], actv[0, :, columns], preferred_element_type=f32)

    def z_send(half, d, n, k):
        part = z_part(wrap(z + d * (n + 1 - k), 8), half)
        slot = Z_BASE[half, d] + k - 1
        if k > 1:
            sent["z", half, d, k - 1].wait_recv()
            part += zr[slot - 1].astype(f32)
        zs[slot] = part.astype(bf16)
        sent["z", half, d, k] = wire.send(zs.at[slot], zr.at[slot], me.at(dz=d), out_z)

    def x_part(dest, half, i):
        columns = rows_at((4 * half + i) * 256, 256)
        return jnp.dot(cott[1, rows_at(dest * 128, 128), :], actv[1, :, columns], preferred_element_type=f32)

    def x_send(half, d, k):
        dest = wrap(x + d * (PAIR_STEPS[half, d] + 1 - k), 4)
        slot = PAIR_BASE[half, d] + k - 1
        if k > 1:
            sent["x", half, d, k - 1].wait_recv()

        def step(i, carry):
            part = x_part(dest, half, i)
            for t in range(2):
                value = part[:, t * 128 : (t + 1) * 128]
                if k > 1:
                    value += xr[slot - 1, 2 * i + t].astype(f32)
                xs[slot, 2 * i + t] = value.astype(bf16)
            return carry

        lax.fori_loop(0, 4, step, 0, unroll=True)
        sent["x", half, d, k] = wire.send(xs.at[slot], xr.at[slot], me.at(dx=d), out_x)

    def y_part(dest, half, i):
        columns = rows_at(((4 * half + i) * 2 + lax.rem(dest, 2)) * 128, 128)
        rows = rows_at(lax.div(dest, 2) * 256, 256)
        return jnp.dot(cott[2, rows, :], actv[2, :, columns], preferred_element_type=f32)

    def y_send(half, d, k):
        dest = wrap(y + d * (PAIR_STEPS[half, d] + 1 - k), 4)
        slot = PAIR_BASE[half, d] + k - 1
        if k > 1:
            sent["y", half, d, k - 1].wait_recv()

        def step(i, carry):
            value = y_part(dest, half, i)
            if k > 1:
                value += yr[slot - 1, i].astype(f32)
            ys[slot, i] = value.astype(bf16)
            return carry

        lax.fori_loop(0, 4, step, 0, unroll=True)
        sent["y", half, d, k] = wire.send(ys.at[slot], yr.at[slot], me.at_y(d), out_y)

    def z_round(k):
        for (half, d), n in Z_STEPS.items():
            if k <= n:
                z_send(half, d, n, k)

    phase("r_prep0")
    prepare(0)
    phase("r_z1")
    z_round(1)
    phase("r_x1")
    prepare(1)
    x_send(0, 1, 1)
    x_send(1, -1, 1)
    phase("r_y1")
    prepare(2)
    y_send(0, 1, 1)
    y_send(1, -1, 1)
    phase("r_xy1b")
    x_send(1, 1, 1)
    x_send(0, -1, 1)
    y_send(1, 1, 1)
    y_send(0, -1, 1)
    phase("r_z2")
    z_round(2)
    phase("r_x2")
    x_send(0, 1, 2)
    x_send(1, -1, 2)
    phase("r_y2")
    y_send(0, 1, 2)
    y_send(1, -1, 2)
    phase("r_z3")
    z_round(3)
    phase("r_z4")
    z_round(4)

    here = rows_at(me.column * 128, 128)

    def slot_matrix(p):
        found, seen, filled = jnp.int32(0), jnp.int32(0), jnp.int32(0)
        for m in range(MATS):
            named = (owners[m] == p).astype(jnp.int32)
            take = named * (seen == c).astype(jnp.int32)
            found, filled, seen = found + take * m, filled + take, seen + named
        return found, filled

    def note(p, carry):
        table[0, p], table[1, p] = slot_matrix(p)
        return carry

    def gather_columns(pieces, target):
        def choose(p, carry):
            found, filled = table[0, p], table[1, p]
            target[p] = (pieces[found].astype(f32) * filled.astype(f32)).astype(bf16)
            return carry

        lax.fori_loop(0, 16, choose, 0, unroll=2)

    phase("r_msend")
    load_momentum.wait()
    load_owners.wait()
    load_starts.wait()
    lax.fori_loop(0, 16, note, 0)
    gather_columns(mb, ms)
    mq[:, here] = ms[me.column]

    phase("r_xlast")
    for half in range(2):
        sent["x", half, 1, PAIR_STEPS[half, 1]].wait_recv()
        sent["x", half, -1, PAIR_STEPS[half, -1]].wait_recv()
        up = PAIR_BASE[half, 1] + PAIR_STEPS[half, 1] - 1
        down = PAIR_BASE[half, -1] + PAIR_STEPS[half, -1] - 1

        def x_last(i, carry, half=half, up=up, down=down):
            part = x_part(x, half, i)
            for t in range(2):
                value = part[:, t * 128 : (t + 1) * 128]
                value += xr[up, 2 * i + t].astype(f32) + xr[down, 2 * i + t].astype(f32)
                x2s[t, 4 * half + i] = value.astype(bf16)
            return carry

        lax.fori_loop(0, 4, x_last, 0, unroll=True)
    copies = []
    for d in (1, 3, 2):
        to = wrap(y + d, 4)
        source = x2s.at[lax.rem(to, 2), :, rows_at(lax.div(to, 2) * 64, 64), :]
        copies.append((source, x2r.at[d - 1], me.at_y(d)))
    sent["x2"] = wire.group(copies, x2r)

    phase("r_ylast")
    for half in range(2):
        sent["y", half, 1, PAIR_STEPS[half, 1]].wait_recv()
        sent["y", half, -1, PAIR_STEPS[half, -1]].wait_recv()
        up = PAIR_BASE[half, 1] + PAIR_STEPS[half, 1] - 1
        down = PAIR_BASE[half, -1] + PAIR_STEPS[half, -1] - 1

        def y_last(i, carry, half=half, up=up, down=down):
            value = y_part(y, half, i) + yr[up, i].astype(f32) + yr[down, i].astype(f32)
            y2s[4 * half + i] = value.astype(bf16)
            return carry

        lax.fori_loop(0, 4, y_last, 0, unroll=True)
    copies = []
    for d in (1, 3, 2):
        to = wrap(x + d, 4)
        copies.append((y2s.at[:, rows_at(to * 64, 64), :], y2r.at[d - 1], me.at(dx=d)))
    sent["y2"] = wire.group(copies, y2r)

    phase("r_zlast")
    for half in range(2):
        last = []
        for d in (1, -1):
            n = Z_STEPS[half, d]
            sent["z", half, d, n].wait_recv()
            last.append(Z_BASE[half, d] + n - 1)
        value = z_part(z, half) + zr[last[0]].astype(f32) + zr[last[1]].astype(f32)
        z2s[half] = value.astype(bf16)
    copies = []
    for d in (1, 3, 2):
        to = wrap(x + d, 4)
        copies.append((z2s.at[:, rows_at(to * 128, 128), :], z2r.at[d - 1], me.at(dx=d)))
    sent["z2"] = wire.group(copies, z2r)
    copies = [(ms.at[p], mq.at[:, here], device) for device, p in me.columns()]
    momentum_to_owner = wire.group(copies, ms.at[:15])

    phase("r_x3")
    sent["x2"].wait_recv()

    def x_third(i, carry):
        value = x2s[yl, i, rows_at(yh * 64, 64), :].astype(f32)
        for d in range(3):
            value += x2r[d, i].astype(f32)
        x3s[i] = value.astype(bf16)
        return carry

    lax.fori_loop(0, 8, x_third, 0, unroll=True)
    copies = [(x3s.at[wrap(z + d, 8)], x3r.at[d - 1], me.at(dz=d)) for d in (4, 3, 5, 2, 6, 1, 7)]
    sent["x3"] = wire.group(copies, x3r)

    phase("r_y3")
    sent["y2"].wait_recv()

    def y_third(i, carry):
        value = y2s[i, rows_at(x * 64, 64), :].astype(f32)
        for d in range(3):
            value += y2r[d, i].astype(f32)
        y3s[i] = value.astype(bf16)
        return carry

    lax.fori_loop(0, 8, y_third, 0, unroll=True)
    copies = [(y3s.at[wrap(z + d, 8)], y3r.at[d - 1], me.at(dz=d)) for d in (4, 3, 5, 2, 6, 1, 7)]
    sent["y3"] = wire.group(copies, y3r)

    phase("r_z3b")
    sent["z2"].wait_recv()
    for t in range(2):
        value = z2s[t, rows_at(x * 128, 128), :].astype(f32)
        for d in range(3):
            value += z2r[d, t].astype(f32)
        z3s[t] = value.astype(bf16)
    copies = []
    for d in (2, 1, 3):
        to = wrap(y + d, 4)
        source = z3s.at[lax.rem(to, 2), rows_at(lax.div(to, 2) * 64, 64), :]
        copies.append((source, z3r.at[d - 1], me.at_y(d)))
    sent["z3"] = wire.group(copies, z3r)

    phase("r_xfin")
    inverse = 1.0 / math.sqrt(TOKENS)
    sqs[c, me.block] = jnp.zeros((8, 128), f32)

    def piece(j, value):
        value = value * inverse
        for kv in range(2):
            block = value[kv * 32 : (kv + 1) * 32]
            gb[6 * c + 2 * j + kv, rows, :] = block.astype(bf16)
            gp[6 * c + 2 * j + kv] = block.astype(bf16)
            total = jnp.sum(block * block, axis=(0, 1), keepdims=True)
            sqs[c, me.block, 2 * j + kv : 2 * j + kv + 1, :] = jnp.broadcast_to(total, (1, 128))

    sent["x3"].wait_recv()
    value = x3s[z].astype(f32)
    for d in range(7):
        value += x3r[d].astype(f32)
    piece(1, value)
    phase("r_yfin")
    sent["y3"].wait_recv()
    value = y3s[z].astype(f32)
    for d in range(7):
        value += y3r[d].astype(f32)
    piece(2, value)
    phase("r_zfin")
    sent["z3"].wait_recv()
    value = z3s[yl, rows_at(yh * 64, 64), :].astype(f32)
    for d in range(3):
        value += z3r[d].astype(f32)
    piece(0, value)

    phase("r_sqsend")
    own = pl.ds(6 * c, 6)
    swap = wire.send(gp.at[own], gp.at[own], me.partner())
    copies = [(sqs.at[c, me.block], sqs.at[c, me.block], me.partner())]
    for dx, dy, core, dz, dl in me.replicas():
        copies.append((sqs.at[c, me.block], sqs.at[c, me.block], (dx, dy, core, dz, dl)))
        copies.append((sqs.at[c, me.block], sqs.at[c, me.block], (dx, dy, 1 - core, dz, dl)))
    squares = wire.group(copies, sq2.at[:15, :8])
    swap.wait_recv()
    gather_columns(gp, us)
    gq[:, here] = us[me.column]
    to_owner = wire.group([(us.at[p], gq.at[:, here], device) for device, p in me.columns()], us.at[:15])
    phase("r_sqw1b")
    squares.wait_recv()
    for core in range(2):
        sq2[me.column, core * 8 : core * 8 + 8] = sum((sqs[core, i] for i in range(1, 8)), sqs[core, 0])
    squares = wire.group(
        [(sq2.at[me.column], sq2.at[me.column], device) for device, _ in me.columns()], sq2.at[:15]
    )
    phase("o_a2a")
    momentum_to_owner.wait_recv()
    to_owner.wait_recv()
    phase("r_sqw2")
    squares.wait_recv()
    totals = sum((sq2[i] for i in range(1, 16)), sq2[0])
    phase("o_choose")

    row = lax.broadcasted_iota(jnp.int32, (16, 128), 0)
    matrix = jnp.where(row >= 8, row - 2, row)
    held = (row < 6) | ((row >= 8) & (row < 14))
    bucket = (matrix >= starts[0]).astype(jnp.int32) + (matrix >= starts[1]).astype(jnp.int32)
    factors = jnp.ones((16, 128), f32)
    for b in range(3):
        inside = held & (bucket == b)
        total = jnp.sum(jnp.where(inside, totals, 0.0), axis=0, keepdims=True)
        members = jnp.sum(inside.astype(f32), axis=0, keepdims=True)
        root_mean = jnp.sqrt(total / (members * (KV * D)) + epsilon)
        factors = jnp.where(inside, jnp.minimum(1.0, clip_level / root_mean), factors)
    f_out[...] = factors
    fac[...] = factors
    mine_is = table[0, me.column]
    factor = fac[pl.ds(mine_is + 2 * (mine_is >= 6).astype(jnp.int32), 1), :]
    for k in range(4):
        cols = slice(k * 512, (k + 1) * 512)
        scaled = factor[:, :1] * gq[:, cols].astype(f32)
        value = scaled + momentum_rate * (momentum_rate * mq[:, cols].astype(f32) + scaled)
        gin[rows, cols] = value.astype(bf16)
    gathered_u = wire.group([(gin.at[rows, :], gin.at[rows, :], device) for device in me.replicas()], gin.at[:224])
    phase("o_ag")
    gathered_u.wait_recv()
    pieces = wire.group(
        [(gb.at[own, rows, :], gb.at[own, rows, :], device) for device in me.replicas()], gb.at[:6, :224, :]
    )

    phase("o_ns")
    orthogonalize(gin, xw, gram)

    phase("o_back")
    copies = [
        (xw.at[rows, rows_at(p * 128, 128)], rb.at[c, me.column], device) for device, p in me.columns()
    ]
    back = wire.group(copies, rb.at[0, :15])
    rb[c, me.column] = xw[rows, here]
    pieces.wait_recv()
    over_g = wire.send(gb.at[own], gb.at[own], me.partner())
    whole = wire.send(xw, o_out.at[c], me.partner())
    store = pltpu.make_async_copy(xw, o_out.at[c], local_sems.at[7])
    store.start()
    back.wait_recv()
    phase("o_over")
    over = wire.send(rb.at[c], rb.at[c], me.partner())
    over.wait_recv()
    for k in range(6):
        m = 6 * c + k
        owner = owners[m]
        slot = jnp.int32(0)
        for j in range(MATS):
            slot = slot + (owners[j] == owner).astype(jnp.int32) * (j < m).astype(jnp.int32)
        ob[m, rows, :] = rb[jnp.minimum(slot, 1), owner]
    phase("o_ag2")
    gathered = wire.group(
        [(ob.at[own, rows, :], ob.at[own, rows, :], device) for device in me.replicas()], ob.at[:6, :224, :]
    )
    over_g.wait_recv()
    store_g = pltpu.make_async_copy(gb, g_out, local_sems.at[8])
    store_g.start()
    gathered.wait_recv()
    phase("o_over2")
    over = wire.send(ob.at[own], ob.at[own], me.partner())
    over.wait_recv()
    out = pltpu.make_async_copy(ob, upd_out, local_sems.at[9])
    out.start()
    phase("o_finish")
    whole.wait_recv()
    store.wait()
    store_g.wait()
    out.wait()
    wire.finish()
    phase.end()


def orthogonalize(xin, xw, gram):
    def squares(i, total):
        value = xin[rows_at(i * 16, 16), :].astype(f32)
        return total + value * value

    total = lax.fori_loop(0, 16, squares, jnp.zeros((16, D), f32))
    norm = jnp.sqrt(jnp.sum(total, axis=(0, 1), keepdims=True))
    scale = 1.0 / (norm + epsilon)

    def start(i, carry):
        block = rows_at(i * 16, 16)
        xw[block, :] = (xin[block, :].astype(f32) * scale).astype(bf16)
        return carry

    lax.fori_loop(0, 16, start, 0)

    def outer(value):
        return lax.dot_general(value, value, (((1,), (1,)), ((), ())), preferred_element_type=f32)

    gram[...] = outer(xw[...])

    def iteration(i, carry):
        rounded = gram[...].astype(bf16)
        square = jnp.dot(rounded, rounded, preferred_element_type=f32)
        mixing = (coef_b * rounded.astype(f32) + coef_c * square).astype(bf16)
        total = None
        for k in range(4):
            cols = slice(k * 512, (k + 1) * 512)
            old = xw[:, cols]
            product = jnp.dot(mixing, old, preferred_element_type=f32)
            new = (coef_a * old.astype(f32) + product).astype(bf16)
            xw[:, cols] = new
            total = outer(new) if k == 0 else total + outer(new)
        gram[...] = total
        return carry

    lax.fori_loop(0, ITERS, iteration, 0)


def stepped(activations, cotangents, momentum, owners, bucket_starts):
    vm = pltpu.VMEM
    operands = (owners, bucket_starts, activations, cotangents, momentum)
    operands = [pltpu.with_memory_space_constraint(a, pltpu.HBM) for a in operands]
    return pl.pallas_call(
        step_kernel,
        out_shape=(
            jax.ShapeDtypeStruct((MATS, KV, 128), bf16),
            jax.ShapeDtypeStruct((16, 128), f32),
            jax.ShapeDtypeStruct((MATS, KV, 128), bf16),
            jax.ShapeDtypeStruct((2, KV, D), bf16),
        ),
        in_specs=[pl.BlockSpec(memory_space=pltpu.HBM)] * 5,
        out_specs=(
            pl.BlockSpec(memory_space=pl.ANY),
            pl.BlockSpec(memory_space=pltpu.VMEM),
            pl.BlockSpec(memory_space=pl.ANY),
            pl.BlockSpec(memory_space=pl.ANY),
        ),
        scratch_shapes=[
            vm((6, 128, 512), bf16), vm((3, 512, 128), bf16), vm((3, 128, D), bf16), vm((3, 256, D), bf16), vm((3, 512, 256), bf16),
            vm((14, 512, 128), bf16), vm((14, 512, 128), bf16),
            vm((6, 8, 128, 128), bf16), vm((6, 8, 128, 128), bf16),
            vm((6, 4, 256, 128), bf16), vm((6, 4, 256, 128), bf16),
            vm((2, 512, 128), bf16), vm((3, 2, 128, 128), bf16), vm((2, 128, 128), bf16), vm((3, 64, 128), bf16),
            vm((2, 8, 128, 128), bf16), vm((3, 8, 64, 128), bf16), vm((8, 64, 128), bf16), vm((7, 64, 128), bf16),
            vm((8, 256, 128), bf16), vm((3, 8, 64, 128), bf16), vm((8, 64, 128), bf16), vm((7, 64, 128), bf16),
            vm((MATS, KV, 128), bf16), vm((MATS, 32, 128), bf16), vm((2, 8, 8, 128), f32), vm((16, 16, 128), f32),
            vm((MATS, 32, 128), f32), vm((16, 32, 128), bf16), vm((16, 32, 128), bf16), vm((16, 128), f32),
            vm((32, D), bf16), vm((32, D), bf16), vm((KV, D), bf16), vm((KV, D), bf16), vm((2, 16, 32, 128), bf16), vm((MATS, KV, 128), bf16),
            vm((KV, KV), f32),
            pltpu.SMEM((MATS,), jnp.int32), pltpu.SMEM((2,), jnp.int32), pltpu.SMEM((2, 16), jnp.int32),
            pltpu.SemaphoreType.DMA((13,)),
            pltpu.SemaphoreType.DMA((OUTLETS,)),
            pltpu.SemaphoreType.DMA((ARRIVALS,)),
        ],
        compiler_params=pltpu.CompilerParams(
            collective_id=0, has_side_effects=True, vmem_limit_bytes=48 * 1024 * 1024
        ),
        name="step",
    )(*operands)


def finish_kernel(factors, g, mom, x, whole, mom_out, update, owned):
    i = pl.program_id(0)
    scale = math.sqrt(max(KV, D))
    for k in range(3):
        m = 3 * i + k
        factor = factors[pl.ds(m + 2 * (m >= 6).astype(jnp.int32), 1), :]
        mom_out[k] = momentum_rate * mom[k] + factor * g[k].astype(f32)
    update[...] = scale * x[...].astype(f32)
    owned[...] = (scale * whole[...].astype(f32)).astype(bf16)


def finished(factors, g, mom, x, whole):
    part = pl.BlockSpec((3, KV, 128), lambda i: (i, 0, 0))
    rows = pl.BlockSpec((2, KV // 4, D), lambda i: (0, i, 0))
    return pl.pallas_call(
        finish_kernel,
        grid=(4,),
        out_shape=(
            jax.ShapeDtypeStruct((MATS, KV, 128), f32),
            jax.ShapeDtypeStruct((MATS, KV, 128), f32),
            jax.ShapeDtypeStruct((2, KV, D), bf16),
        ),
        in_specs=[pl.BlockSpec((16, 128), lambda i: (0, 0)), part, part, part, rows],
        out_specs=(part, part, rows),
        compiler_params=pltpu.CompilerParams(vmem_limit_bytes=16 * 1024 * 1024),
        name="finish",
    )(factors, g, mom, x, whole)


def per_device(activations, cotangents, momentum, owners, bucket_starts):
    g, factors, x, whole = stepped(activations, cotangents, momentum, owners, bucket_starts)
    return finished(factors, g, momentum, x, whole)


def solution(mesh):
    torus = Mesh(
        mesh.devices.reshape(4, 2, 2, 8, 2), ("rep_0", "rep_1", "rep_2", "shard_0", "shard_1")
    )
    return jax.shard_map(
        per_device,
        mesh=torus,
        in_specs=(
            P(None, REP_SHARD, None),
            P(None, REP_SHARD, None),
            P(None, None, SHARD),
            P(),
            P(),
        ),
        out_specs=(P(None, None, SHARD), P(None, None, SHARD), P(SHARD, None, None)),
        check_vma=False,
    )
```

time: 130 us -> 105 us (0.81)
  Pallas kernels: 120 us -> 104 us
  other arithmetic: 8.07 us -> 0 us
    pallas_call x2, Pallas kernels: 120 us -> 104 us  [the longest x1 101 us: stepped(): pl.pallas_call(step_kernel, out_shape=(jax.ShapeDtypeStruct((MATS, KV, 12...]
    convert_element_type x2 -> x0, other arithmetic: 6.49 us -> none  [the longest x1 3.52 us: per_device(): owned = (update_scale * whole.astype(f32)).astype(bf16)]
    mul x1 -> x0, other arithmetic: 1.3 us -> none  [per_device(): update = update_scale * returned.astype(f32)]
where the time goes in v2:
time: 105 us
  Pallas kernels  104 us (99%)
    pallas_call x1, Pallas kernels, stepped(): pl.pallas_call(step_kernel, out_shape=(jax.ShapeDtypeStruct((MATS, KV, 12...  101 us
    pallas_call x1, Pallas kernels, finished(): pl.pallas_call(finish_kernel, grid=(4,), out_shape=(jax.ShapeDtypeStruct(...  2.88 us

profile of v2, /device:TPU:1, one launch (start us, length us, event | category | flops | bytes accessed | tf_op | source)
XLA Modules:
  0.0 104.8 jit_solution(8471684872508552610)
XLA Ops:
  0.6 0.0 copy-start
  0.6 101.3 %step.1 = (bf16[12,256,128]{2,1,0:T(8,128)(2,1)S(1)}, f32[16,128]{1,0:T(8,128)S(1)}, bf16[12,256,128]{2,1,0:T(8,128)(2,1)S(1)}, bf16[2,256,2048]{2,1,0:T(8,128)(2,1)S(1)}) custom-call(s32[12]{0:T(128)} %owners_in.1, s32[2]{0:T(128)} %starts_in.1, bf16[6,128,2048]{2,1,0:T(8,128)(2,1)} %act.1, bf16[6,128,512]{2,1,0:T(8,128)(2,1)} %cot.1, f32[12,256,128]{2,1,0:T(8,128)} %mom.3), custom_call_target="tpu_custom_call" | custom-call | tf_op jit(solution)/shard_map/step/pallas_call | solution.py:637
  101.9 0.0 copy-done
  101.9 2.9 %finish.1 = (f32[12,256,128]{2,1,0:T(8,128)}, f32[12,256,128]{2,1,0:T(8,128)}, bf16[2,256,2048]{2,1,0:T(8,128)(2,1)}) custom-call(f32[16,128]{1,0:T(8,128)S(1)} %get-tuple-element.7.factors, bf16[12,256,128]{2,1,0:T(8,128)(2,1)S(1)} %get-tuple-element.8.g, f32[12,256,128]{2,1,0:T(8,128)S(1)} %copy-done, bf16[12,256,128]{2,1,0:T(8,128)(2,1)S(1)} %get-tuple-element.9.x, ...), custom_call_target="tpu_custom_call" | custom-call | tf_op jit(solution)/shard_map/finish/pallas_call | solution.py:690
Async XLA Ops:
  0.6 101.3 %copy-start = (f32[12,256,128]{2,1,0:T(8,128)S(1)}, f32[12,256,128]{2,1,0:T(8,128)}, u32[]{:S(2)}) copy-start(f32[12,256,128]{2,1,0:T(8,128)} %mom.3) | copy-start | bytes 4718596

commit v3 on v2

--- a/solution.py
+++ b/solution.py
@@ -54,6 +54,11 @@
     def partner(self):
         return (self.x, self.yh, 1 - self.c, self.z, self.yl)
 
+    def near(self, dx, dy, dc, dz):
+        y = wrap(self.y + dy, 4)
+        core = 1 - self.c if dc else self.c
+        return (wrap(self.x + dx, 4), lax.div(y, 2), core, wrap(self.z + dz, 8), lax.rem(y, 2))
+
     def replicas(self):
         for dx in range(4):
             for dyh in range(2):
@@ -153,7 +158,7 @@
 Z_BASE = {(0, 1): 0, (1, -1): 4, (1, 1): 8, (0, -1): 11}
 PAIR_BASE = {(0, 1): 0, (1, -1): 2, (1, 1): 4, (0, -1): 5}
 PAIR_STEPS = {(0, 1): 2, (1, -1): 2, (1, 1): 1, (0, -1): 1}
-OUTLETS, ARRIVALS = 24, 51
+OUTLETS, ARRIVALS = 29, 56
 
 
 def step_kernel(
@@ -177,7 +182,7 @@
         loads_out[j].start()
         loads[j].start()
     rows = rows_at(me.block * 32, 32)
-    load_momentum = pltpu.make_async_copy(mom.at[:, rows, :], mb, local_sems.at[12])
+    load_momentum = pltpu.make_async_copy(mom.at[:, rows_at(x * 64, 64), :], mb, local_sems.at[12])
     load_momentum.start()
     load_owners = pltpu.make_async_copy(owners_in, owners, local_sems.at[10])
     load_starts = pltpu.make_async_copy(starts_in, starts, local_sems.at[11])
@@ -185,13 +190,9 @@
     load_starts.start()
 
     phase("r_greet")
-    devices = [me.partner()]
-    devices += [me.at(dx=d) for d in range(1, 4)]
-    devices += [me.at_y(d) for d in range(1, 4)]
-    devices += [(wrap(x + d, 4), 1 - yh, c, z, yl) for d in range(1, 4)]
-    devices += [(dx, dy, 1 - c, dz, dl) for dx, dy, _, dz, dl in me.replicas()]
-    devices += [me.at(dz=d) for d in range(1, 8)]
-    devices += [(x, yh, c, wrap(z + d, 8), 1 - yl) for d in range(1, 8)]
+    plane = [(dx, dy, dc) for dx in range(4) for dy in range(4) for dc in range(2) if dx or dy or dc]
+    devices = [me.near(dx, dy, dc, 0) for dx, dy, dc in plane]
+    devices += [me.near(0, dy, 0, dz) for dy in range(4) for dz in range(1, 8)]
     signal_all(devices)
 
     def turn(source, store, inner_is_x):
@@ -204,7 +205,7 @@
                     store(to, turned[at : at + 32, :])
 
     load_cot.wait()
-    for j in range(3):
+    for j in (1, 2, 0):
 
         def store_out(to, value, j=j):
             cout[j, to : to + 32, :] = value
@@ -220,14 +221,12 @@
     phase("r_swap")
     out_cot, out_act = wire.outlet(cout), wire.outlet(aout)
     out_x, out_y, out_z = wire.outlet(xs), wire.outlet(ys), wire.outlet(zs)
-    swaps = []
-    for j in range(3):
+    swaps = {}
+    for j in (1, 2, 0):
         loads_out[j].wait()
-        swaps.append(
-            (
-                wire.send(cout.at[j], cott.at[j, :, mine], me.partner(), out_cot),
-                wire.send(aout.at[j], actv.at[j, mine], me.partner(), out_act),
-            )
+        swaps[j] = (
+            wire.send(cout.at[j], cott.at[j, :, mine], me.partner(), out_cot),
+            wire.send(aout.at[j], actv.at[j, mine], me.partner(), out_act),
         )
 
     def prepare(j):
@@ -299,17 +298,17 @@
                 z_send(half, d, n, k)
 
     phase("r_prep0")
-    prepare(0)
-    phase("r_z1")
-    z_round(1)
+    prepare(1)
     phase("r_x1")
-    prepare(1)
     x_send(0, 1, 1)
     x_send(1, -1, 1)
     phase("r_y1")
     prepare(2)
     y_send(0, 1, 1)
     y_send(1, -1, 1)
+    phase("r_z1")
+    prepare(0)
+    z_round(1)
     phase("r_xy1b")
     x_send(1, 1, 1)
     x_send(0, -1, 1)
@@ -461,7 +460,7 @@
 
     phase("r_xfin")
     inverse = 1.0 / math.sqrt(TOKENS)
-    sqs[c, me.block] = jnp.zeros((8, 128), f32)
+    sqs[z] = jnp.zeros((8, 128), f32)
 
     def piece(j, value):
         value = value * inverse
@@ -470,7 +469,7 @@
             gb[6 * c + 2 * j + kv, rows, :] = block.astype(bf16)
             gp[6 * c + 2 * j + kv] = block.astype(bf16)
             total = jnp.sum(block * block, axis=(0, 1), keepdims=True)
-            sqs[c, me.block, 2 * j + kv : 2 * j + kv + 1, :] = jnp.broadcast_to(total, (1, 128))
+            sqs[z, 2 * j + kv : 2 * j + kv + 1, :] = jnp.broadcast_to(total, (1, 128))
 
     sent["x3"].wait_recv()
     value = x3s[z].astype(f32)
@@ -492,29 +491,33 @@
 
     phase("r_sqsend")
     own = pl.ds(6 * c, 6)
+    squares = wire.group([(sqs.at[z], sqs.at[z], me.at(dz=d)) for d in (4, 3, 5, 2, 6, 1, 7)], sqs.at[:7])
     swap = wire.send(gp.at[own], gp.at[own], me.partner())
-    copies = [(sqs.at[c, me.block], sqs.at[c, me.block], me.partner())]
-    for dx, dy, core, dz, dl in me.replicas():
-        copies.append((sqs.at[c, me.block], sqs.at[c, me.block], (dx, dy, core, dz, dl)))
-        copies.append((sqs.at[c, me.block], sqs.at[c, me.block], (dx, dy, 1 - core, dz, dl)))
-    squares = wire.group(copies, sq2.at[:15, :8])
     swap.wait_recv()
     gather_columns(gp, us)
-    gq[:, here] = us[me.column]
-    to_owner = wire.group([(us.at[p], gq.at[:, here], device) for device, p in me.columns()], us.at[:15])
+    half = rows_at(yh * 32, 32)
+    gq[half, here] = us[me.column]
+    copies = []
+    for dz in (4, 3, 5, 2, 6, 1, 7, 0):
+        for dy in (2, 1, 3, 0):
+            if dz or dy:
+                device = me.near(0, dy, 0, dz)
+                copies.append((us.at[2 * device[3] + device[4]], gq.at[half, here], device))
+    to_owner = wire.group(copies, rb.at[:31])
     phase("r_sqw1b")
     squares.wait_recv()
-    for core in range(2):
-        sq2[me.column, core * 8 : core * 8 + 8] = sum((sqs[core, i] for i in range(1, 8)), sqs[core, 0])
+    spot = c * 16 + 4 * x + y
+    sq2[spot] = sum((sqs[i] for i in range(1, 8)), sqs[0])
     squares = wire.group(
-        [(sq2.at[me.column], sq2.at[me.column], device) for device, _ in me.columns()], sq2.at[:15]
+        [(sq2.at[spot], sq2.at[spot], me.near(dx, dy, dc, 0)) for dx, dy, dc in plane], sq2.at[:31]
     )
+    phase("r_sqw2")
+    squares.wait_recv()
+    totals = [sum((sq2[k * 16 + i] for i in range(1, 16)), sq2[k * 16]) for k in range(2)]
+    totals = jnp.concatenate(totals, axis=0)
     phase("o_a2a")
     momentum_to_owner.wait_recv()
     to_owner.wait_recv()
-    phase("r_sqw2")
-    squares.wait_recv()
-    totals = sum((sq2[i] for i in range(1, 16)), sq2[0])
     phase("o_choose")
 
     row = lax.broadcasted_iota(jnp.int32, (16, 128), 0)
@@ -536,10 +539,24 @@
         cols = slice(k * 512, (k + 1) * 512)
         scaled = factor[:, :1] * gq[:, cols].astype(f32)
         value = scaled + momentum_rate * (momentum_rate * mq[:, cols].astype(f32) + scaled)
-        gin[rows, cols] = value.astype(bf16)
-    gathered_u = wire.group([(gin.at[rows, :], gin.at[rows, :], device) for device in me.replicas()], gin.at[:224])
+        gin[rows_at(x * 64, 64), cols] = value.astype(bf16)
+
     phase("o_ag")
-    gathered_u.wait_recv()
+
+    def part(dx, h):
+        return gin.at[rows_at(wrap(x + dx, 4) * 64 + 32 * h, 32), :]
+
+    ahead, behind = me.at(dx=1), me.at(dx=-1)
+    first_up = wire.send(part(0, 0), part(0, 0), ahead)
+    first_down = wire.send(part(0, 1), part(0, 1), behind)
+    second_up = wire.send(part(0, 1), part(0, 1), ahead)
+    second_down = wire.send(part(0, 0), part(0, 0), behind)
+    first_up.wait_recv()
+    third_up = wire.send(part(-1, 0), part(-1, 0), ahead)
+    first_down.wait_recv()
+    third_down = wire.send(part(1, 1), part(1, 1), behind)
+    for copy in (second_up, second_down, third_up, third_down):
+        copy.wait_recv()
     pieces = wire.group(
         [(gb.at[own, rows, :], gb.at[own, rows, :], device) for device in me.replicas()], gb.at[:6, :224, :]
     )
@@ -549,10 +566,10 @@
 
     phase("o_back")
     copies = [
-        (xw.at[rows, rows_at(p * 128, 128)], rb.at[c, me.column], device) for device, p in me.columns()
+        (xw.at[rows, rows_at(p * 128, 128)], rb.at[c * 16 + me.column], device) for device, p in me.columns()
     ]
-    back = wire.group(copies, rb.at[0, :15])
-    rb[c, me.column] = xw[rows, here]
+    back = wire.group(copies, rb.at[:15])
+    rb[c * 16 + me.column] = xw[rows, here]
     pieces.wait_recv()
     over_g = wire.send(gb.at[own], gb.at[own], me.partner())
     whole = wire.send(xw, o_out.at[c], me.partner())
@@ -560,7 +577,8 @@
     store.start()
     back.wait_recv()
     phase("o_over")
-    over = wire.send(rb.at[c], rb.at[c], me.partner())
+    slots = pl.ds(c * 16, 16)
+    over = wire.send(rb.at[slots], rb.at[slots], me.partner())
     over.wait_recv()
     for k in range(6):
         m = 6 * c + k
@@ -568,7 +586,7 @@
         slot = jnp.int32(0)
         for j in range(MATS):
             slot = slot + (owners[j] == owner).astype(jnp.int32) * (j < m).astype(jnp.int32)
-        ob[m, rows, :] = rb[jnp.minimum(slot, 1), owner]
+        ob[m, rows, :] = rb[jnp.minimum(slot, 1) * 16 + owner]
     phase("o_ag2")
     gathered = wire.group(
         [(ob.at[own, rows, :], ob.at[own, rows, :], device) for device in me.replicas()], ob.at[:6, :224, :]
@@ -592,42 +610,38 @@
 
 
 def orthogonalize(xin, xw, gram):
-    def squares(i, total):
-        value = xin[rows_at(i * 16, 16), :].astype(f32)
-        return total + value * value
-
-    total = lax.fori_loop(0, 16, squares, jnp.zeros((16, D), f32))
-    norm = jnp.sqrt(jnp.sum(total, axis=(0, 1), keepdims=True))
-    scale = 1.0 / (norm + epsilon)
-
-    def start(i, carry):
-        block = rows_at(i * 16, 16)
-        xw[block, :] = (xin[block, :].astype(f32) * scale).astype(bf16)
-        return carry
-
-    lax.fori_loop(0, 16, start, 0)
-
     def outer(value):
         return lax.dot_general(value, value, (((1,), (1,)), ((), ())), preferred_element_type=f32)
 
-    gram[...] = outer(xw[...])
-
-    def iteration(i, carry):
+    def iteration(x_of, last):
         rounded = gram[...].astype(bf16)
         square = jnp.dot(rounded, rounded, preferred_element_type=f32)
         mixing = (coef_b * rounded.astype(f32) + coef_c * square).astype(bf16)
         total = None
         for k in range(4):
             cols = slice(k * 512, (k + 1) * 512)
-            old = xw[:, cols]
+            old = x_of(cols)
             product = jnp.dot(mixing, old, preferred_element_type=f32)
             new = (coef_a * old.astype(f32) + product).astype(bf16)
             xw[:, cols] = new
-            total = outer(new) if k == 0 else total + outer(new)
-        gram[...] = total
+            if not last:
+                total = outer(new) if k == 0 else total + outer(new)
+        if not last:
+            gram[...] = total
+
+    first = outer(xin[...])
+    diagonal = lax.broadcasted_iota(jnp.int32, (KV, KV), 0) == lax.broadcasted_iota(jnp.int32, (KV, KV), 1)
+    norm = jnp.sqrt(jnp.sum(jnp.where(diagonal, first, 0.0), axis=(0, 1), keepdims=True))
+    scale = 1.0 / (norm + epsilon)
+    gram[...] = first * scale * scale
+    iteration(lambda cols: (xin[:, cols].astype(f32) * scale).astype(bf16), False)
+
+    def middle(i, carry):
+        iteration(lambda cols: xw[:, cols], False)
         return carry
 
-    lax.fori_loop(0, ITERS, iteration, 0)
+    lax.fori_loop(0, ITERS - 2, middle, 0)
+    iteration(lambda cols: xw[:, cols], True)
 
 
 def stepped(activations, cotangents, momentum, owners, bucket_starts):
@@ -657,9 +671,9 @@
             vm((2, 512, 128), bf16), vm((3, 2, 128, 128), bf16), vm((2, 128, 128), bf16), vm((3, 64, 128), bf16),
             vm((2, 8, 128, 128), bf16), vm((3, 8, 64, 128), bf16), vm((8, 64, 128), bf16), vm((7, 64, 128), bf16),
             vm((8, 256, 128), bf16), vm((3, 8, 64, 128), bf16), vm((8, 64, 128), bf16), vm((7, 64, 128), bf16),
-            vm((MATS, KV, 128), bf16), vm((MATS, 32, 128), bf16), vm((2, 8, 8, 128), f32), vm((16, 16, 128), f32),
-            vm((MATS, 32, 128), f32), vm((16, 32, 128), bf16), vm((16, 32, 128), bf16), vm((16, 128), f32),
-            vm((32, D), bf16), vm((32, D), bf16), vm((KV, D), bf16), vm((KV, D), bf16), vm((2, 16, 32, 128), bf16), vm((MATS, KV, 128), bf16),
+            vm((MATS, KV, 128), bf16), vm((MATS, 32, 128), bf16), vm((8, 8, 128), f32), vm((32, 8, 128), f32),
+            vm((MATS, 64, 128), f32), vm((16, 32, 128), bf16), vm((16, 64, 128), bf16), vm((16, 128), f32),
+            vm((64, D), bf16), vm((64, D), bf16), vm((KV, D), bf16), vm((KV, D), bf16), vm((32, 32, 128), bf16), vm((MATS, KV, 128), bf16),
             vm((KV, KV), f32),
             pltpu.SMEM((MATS,), jnp.int32), pltpu.SMEM((2,), jnp.int32), pltpu.SMEM((2, 16), jnp.int32),
             pltpu.SemaphoreType.DMA((13,)),

time: 105 us -> 101 us (0.962)
  Pallas kernels: 104 us -> 100 us
    pallas_call x1, Pallas kernels: 101 us -> 97.3 us  [stepped(): pl.pallas_call(step_kernel, out_shape=(jax.ShapeDtypeStruct((MATS, KV, 12...]
where the time goes in v3:
time: 101 us
  Pallas kernels  100 us (99%)
    pallas_call x1, Pallas kernels, stepped(): pl.pallas_call(step_kernel, out_shape=(jax.ShapeDtypeStruct((MATS, KV, 12...  97.3 us
    pallas_call x1, Pallas kernels, finished(): pl.pallas_call(finish_kernel, grid=(4,), out_shape=(jax.ShapeDtypeStruct(...  2.88 us

profile of v3, /device:TPU:1, one launch (start us, length us, event | category | flops | bytes accessed | tf_op | source)
XLA Modules:
  0.0 100.8 jit_solution(11853771681048779514)
XLA Ops:
  0.6 0.0 copy-start
  0.6 97.3 %step.1 = (bf16[12,256,128]{2,1,0:T(8,128)(2,1)S(1)}, f32[16,128]{1,0:T(8,128)S(1)}, bf16[12,256,128]{2,1,0:T(8,128)(2,1)S(1)}, bf16[2,256,2048]{2,1,0:T(8,128)(2,1)S(1)}) custom-call(s32[12]{0:T(128)} %owners_in.1, s32[2]{0:T(128)} %starts_in.1, bf16[6,128,2048]{2,1,0:T(8,128)(2,1)} %act.1, bf16[6,128,512]{2,1,0:T(8,128)(2,1)} %cot.1, f32[12,256,128]{2,1,0:T(8,128)} %mom.3), custom_call_target="tpu_custom_call" | custom-call | tf_op jit(solution)/shard_map/step/pallas_call | solution.py:651
  98.0 0.0 copy-done
  98.0 2.9 %finish.1 = (f32[12,256,128]{2,1,0:T(8,128)}, f32[12,256,128]{2,1,0:T(8,128)}, bf16[2,256,2048]{2,1,0:T(8,128)(2,1)}) custom-call(f32[16,128]{1,0:T(8,128)S(1)} %get-tuple-element.7.factors, bf16[12,256,128]{2,1,0:T(8,128)(2,1)S(1)} %get-tuple-element.8.g, f32[12,256,128]{2,1,0:T(8,128)S(1)} %copy-done, bf16[12,256,128]{2,1,0:T(8,128)(2,1)S(1)} %get-tuple-element.9.x, ...), custom_call_target="tpu_custom_call" | custom-call | tf_op jit(solution)/shard_map/finish/pallas_call | solution.py:704
Async XLA Ops:
  0.6 97.3 %copy-start = (f32[12,256,128]{2,1,0:T(8,128)S(1)}, f32[12,256,128]{2,1,0:T(8,128)}, u32[]{:S(2)}) copy-start(f32[12,256,128]{2,1,0:T(8,128)} %mom.3) | copy-start | bytes 4718596

commit v4 on v3

--- a/solution.py
+++ b/solution.py
@@ -60,10 +60,11 @@
         return (wrap(self.x + dx, 4), lax.div(y, 2), core, wrap(self.z + dz, 8), lax.rem(y, 2))
 
     def replicas(self):
-        for dx in range(4):
-            for dyh in range(2):
-                if dx or dyh:
-                    yield (wrap(self.x + dx, 4), lax.rem(self.yh + dyh, 2), self.c, self.z, self.yl)
+        for dx, dyh in self.offsets():
+            yield (wrap(self.x + dx, 4), lax.rem(self.yh + dyh, 2), self.c, self.z, self.yl)
+
+    def offsets(self):
+        return ((1, 0), (3, 0), (0, 1), (2, 0), (1, 1), (3, 1), (2, 1))
 
     def columns_at(self, dz):
         for dyl in range(2):
@@ -158,7 +159,7 @@
 Z_BASE = {(0, 1): 0, (1, -1): 4, (1, 1): 8, (0, -1): 11}
 PAIR_BASE = {(0, 1): 0, (1, -1): 2, (1, 1): 4, (0, -1): 5}
 PAIR_STEPS = {(0, 1): 2, (1, -1): 2, (1, 1): 1, (0, -1): 1}
-OUTLETS, ARRIVALS = 29, 56
+OUTLETS, ARRIVALS = 39, 67
 
 
 def step_kernel(
@@ -224,10 +225,13 @@
     swaps = {}
     for j in (1, 2, 0):
         loads_out[j].wait()
-        swaps[j] = (
-            wire.send(cout.at[j], cott.at[j, :, mine], me.partner(), out_cot),
-            wire.send(aout.at[j], actv.at[j, mine], me.partner(), out_act),
-        )
+        swaps[j] = [wire.send(cout.at[j], cott.at[j, :, mine], me.partner(), out_cot)]
+        parts = 2 if j == 1 else 1
+        for k in range(parts):
+            cols = pl.ds(k * (D // parts), D // parts)
+            swaps[j].append(
+                wire.send(aout.at[j, :, cols], actv.at[j, mine, cols], me.partner(), out_act)
+            )
 
     def prepare(j):
         loads[j].wait()
@@ -292,15 +296,16 @@
         lax.fori_loop(0, 4, step, 0, unroll=True)
         sent["y", half, d, k] = wire.send(ys.at[slot], yr.at[slot], me.at_y(d), out_y)
 
-    def z_round(k):
+    def z_round(k, long=None):
         for (half, d), n in Z_STEPS.items():
-            if k <= n:
+            if k <= n and long in (None, n == 4):
                 z_send(half, d, n, k)
 
     phase("r_prep0")
     prepare(1)
     phase("r_x1")
     x_send(0, 1, 1)
+    swaps[1][2].wait_recv()
     x_send(1, -1, 1)
     phase("r_y1")
     prepare(2)
@@ -314,19 +319,6 @@
     x_send(0, -1, 1)
     y_send(1, 1, 1)
     y_send(0, -1, 1)
-    phase("r_z2")
-    z_round(2)
-    phase("r_x2")
-    x_send(0, 1, 2)
-    x_send(1, -1, 2)
-    phase("r_y2")
-    y_send(0, 1, 2)
-    y_send(1, -1, 2)
-    phase("r_z3")
-    z_round(3)
-    phase("r_z4")
-    z_round(4)
-
     here = rows_at(me.column * 128, 128)
 
     def slot_matrix(p):
@@ -357,7 +349,38 @@
     gather_columns(mb, ms)
     mq[:, here] = ms[me.column]
 
+    phase("r_z2")
+    z_round(2, True)
+    phase("r_x2")
+    x_send(0, 1, 2)
+    x_send(1, -1, 2)
+    phase("r_y2")
+    y_send(0, 1, 2)
+    y_send(1, -1, 2)
+    phase("r_z2b")
+    z_round(2, False)
+    phase("r_z3")
+    z_round(3, True)
+    z_round(3, False)
+    phase("r_z4")
+    z_round(4)
+    copies = [(ms.at[p], mq.at[:, here], device) for device, p in me.columns()]
+    momentum_to_owner = wire.group(copies, ms.at[:15])
+
     phase("r_xlast")
+    def turned_z(to):
+        return wrap(to - z - 2, 8)
+
+    def third(second, buffer, arrived, here, store):
+        for e in range(4 * second, 4 * second + 4):
+            value = here(e).astype(f32)
+            for d in range(3):
+                value += arrived[second, d, e % 4].astype(f32)
+            buffer[e] = value.astype(bf16)
+        places = (2, 1, 3, 0) if second == 0 else (4, 7, 5)
+        copies = [(buffer.at[e], store.at[e], me.at(dz=e + 2)) for e in places]
+        return wire.group(copies, store.at[: len(places)])
+
     for half in range(2):
         sent["x", half, 1, PAIR_STEPS[half, 1]].wait_recv()
         sent["x", half, -1, PAIR_STEPS[half, -1]].wait_recv()
@@ -369,16 +392,17 @@
             for t in range(2):
                 value = part[:, t * 128 : (t + 1) * 128]
                 value += xr[up, 2 * i + t].astype(f32) + xr[down, 2 * i + t].astype(f32)
-                x2s[t, 4 * half + i] = value.astype(bf16)
+                x2s[t, turned_z(4 * half + i)] = value.astype(bf16)
             return carry
 
         lax.fori_loop(0, 4, x_last, 0, unroll=True)
-    copies = []
-    for d in (1, 3, 2):
-        to = wrap(y + d, 4)
-        source = x2s.at[lax.rem(to, 2), :, rows_at(lax.div(to, 2) * 64, 64), :]
-        copies.append((source, x2r.at[d - 1], me.at_y(d)))
-    sent["x2"] = wire.group(copies, x2r)
+    for second in range(2):
+        copies = []
+        for d in (1, 3, 2):
+            to = wrap(y + d, 4)
+            source = x2s.at[lax.rem(to, 2), pl.ds(4 * second, 4), rows_at(lax.div(to, 2) * 64, 64), :]
+            copies.append((source, x2r.at[second, d - 1], me.at_y(d)))
+        sent["x2", second] = wire.group(copies, x2r.at[second])
 
     phase("r_ylast")
     for half in range(2):
@@ -389,15 +413,16 @@
 
         def y_last(i, carry, half=half, up=up, down=down):
             value = y_part(y, half, i) + yr[up, i].astype(f32) + yr[down, i].astype(f32)
-            y2s[4 * half + i] = value.astype(bf16)
+            y2s[turned_z(4 * half + i)] = value.astype(bf16)
             return carry
 
         lax.fori_loop(0, 4, y_last, 0, unroll=True)
-    copies = []
-    for d in (1, 3, 2):
-        to = wrap(x + d, 4)
-        copies.append((y2s.at[:, rows_at(to * 64, 64), :], y2r.at[d - 1], me.at(dx=d)))
-    sent["y2"] = wire.group(copies, y2r)
+    for second in range(2):
+        copies = []
+        for d in (1, 3, 2):
+            source = y2s.at[pl.ds(4 * second, 4), rows_at(wrap(x + d, 4) * 64, 64), :]
+            copies.append((source, y2r.at[second, d - 1], me.at(dx=d)))
+        sent["y2", second] = wire.group(copies, y2r.at[second])
 
     phase("r_zlast")
     for half in range(2):
@@ -413,50 +438,36 @@
         to = wrap(x + d, 4)
         copies.append((z2s.at[:, rows_at(to * 128, 128), :], z2r.at[d - 1], me.at(dx=d)))
     sent["z2"] = wire.group(copies, z2r)
-    copies = [(ms.at[p], mq.at[:, here], device) for device, p in me.columns()]
-    momentum_to_owner = wire.group(copies, ms.at[:15])
-
-    phase("r_x3")
-    sent["x2"].wait_recv()
-
-    def x_third(i, carry):
-        value = x2s[yl, i, rows_at(yh * 64, 64), :].astype(f32)
-        for d in range(3):
-            value += x2r[d, i].astype(f32)
-        x3s[i] = value.astype(bf16)
-        return carry
-
-    lax.fori_loop(0, 8, x_third, 0, unroll=True)
-    copies = [(x3s.at[wrap(z + d, 8)], x3r.at[d - 1], me.at(dz=d)) for d in (4, 3, 5, 2, 6, 1, 7)]
-    sent["x3"] = wire.group(copies, x3r)
-
-    phase("r_y3")
-    sent["y2"].wait_recv()
-
-    def y_third(i, carry):
-        value = y2s[i, rows_at(x * 64, 64), :].astype(f32)
-        for d in range(3):
-            value += y2r[d, i].astype(f32)
-        y3s[i] = value.astype(bf16)
-        return carry
-
-    lax.fori_loop(0, 8, y_third, 0, unroll=True)
-    copies = [(y3s.at[wrap(z + d, 8)], y3r.at[d - 1], me.at(dz=d)) for d in (4, 3, 5, 2, 6, 1, 7)]
-    sent["y3"] = wire.group(copies, y3r)
-
-    phase("r_z3b")
-    sent["z2"].wait_recv()
-    for t in range(2):
-        value = z2s[t, rows_at(x * 128, 128), :].astype(f32)
-        for d in range(3):
-            value += z2r[d, t].astype(f32)
-        z3s[t] = value.astype(bf16)
-    copies = []
-    for d in (2, 1, 3):
-        to = wrap(y + d, 4)
-        source = z3s.at[lax.rem(to, 2), rows_at(lax.div(to, 2) * 64, 64), :]
-        copies.append((source, z3r.at[d - 1], me.at_y(d)))
-    sent["z3"] = wire.group(copies, z3r)
+    def z_second():
+        phase("r_z3b")
+        sent["z2"].wait_recv()
+        for t in range(2):
+            value = z2s[t, rows_at(x * 128, 128), :].astype(f32)
+            for d in range(3):
+                value += z2r[d, t].astype(f32)
+            z3s[t] = value.astype(bf16)
+        copies = []
+        for d in (2, 1, 3):
+            to = wrap(y + d, 4)
+            source = z3s.at[lax.rem(to, 2), rows_at(lax.div(to, 2) * 64, 64), :]
+            copies.append((source, z3r.at[d - 1], me.at_y(d)))
+        sent["z3"] = wire.group(copies, z3r)
+
+    def x_here(e):
+        return x2s[yl, e, rows_at(yh * 64, 64), :]
+
+    def y_here(e):
+        return y2s[e, rows_at(x * 64, 64), :]
+
+    for second in range(2):
+        phase("r_x3" + "ab"[second])
+        sent["x2", second].wait_recv()
+        sent["x3", second] = third(second, x3s, x2r, x_here, x3r)
+        phase("r_y3" + "ab"[second])
+        sent["y2", second].wait_recv()
+        sent["y3", second] = third(second, y3s, y2r, y_here, y3r)
+        if second == 0:
+            z_second()
 
     phase("r_xfin")
     inverse = 1.0 / math.sqrt(TOKENS)
@@ -471,16 +482,18 @@
             total = jnp.sum(block * block, axis=(0, 1), keepdims=True)
             sqs[z, 2 * j + kv : 2 * j + kv + 1, :] = jnp.broadcast_to(total, (1, 128))
 
-    sent["x3"].wait_recv()
-    value = x3s[z].astype(f32)
-    for d in range(7):
-        value += x3r[d].astype(f32)
+    sent["x3", 0].wait_recv()
+    sent["x3", 1].wait_recv()
+    value = x3s[6].astype(f32)
+    for e in (0, 1, 2, 3, 4, 5, 7):
+        value += x3r[e].astype(f32)
     piece(1, value)
     phase("r_yfin")
-    sent["y3"].wait_recv()
-    value = y3s[z].astype(f32)
-    for d in range(7):
-        value += y3r[d].astype(f32)
+    sent["y3", 0].wait_recv()
+    sent["y3", 1].wait_recv()
+    value = y3s[6].astype(f32)
+    for e in (0, 1, 2, 3, 4, 5, 7):
+        value += y3r[e].astype(f32)
     piece(2, value)
     phase("r_zfin")
     sent["z3"].wait_recv()
@@ -588,16 +601,19 @@
             slot = slot + (owners[j] == owner).astype(jnp.int32) * (j < m).astype(jnp.int32)
         ob[m, rows, :] = rb[jnp.minimum(slot, 1) * 16 + owner]
     phase("o_ag2")
-    gathered = wire.group(
-        [(ob.at[own, rows, :], ob.at[own, rows, :], device) for device in me.replicas()], ob.at[:6, :224, :]
-    )
+    gathered = [wire.send(ob.at[own, rows, :], ob.at[own, rows, :], device) for device in me.replicas()]
+    onward = wire.opened(ob.at[:6])
+    wire.join(onward, [(ob.at[own, rows, :], ob.at[own, rows, :], me.partner())])
     over_g.wait_recv()
     store_g = pltpu.make_async_copy(gb, g_out, local_sems.at[8])
     store_g.start()
-    gathered.wait_recv()
+    for copy, (dx, dyh) in zip(gathered, me.offsets(), strict=True):
+        copy.wait_recv()
+        block = 2 * wrap(x - dx, 4) + lax.rem(yh + dyh, 2)
+        arrived = ob.at[own, rows_at(block * 32, 32), :]
+        wire.join(onward, [(arrived, arrived, me.partner())])
     phase("o_over2")
-    over = wire.send(ob.at[own], ob.at[own], me.partner())
-    over.wait_recv()
+    onward.wait_recv()
     out = pltpu.make_async_copy(ob, upd_out, local_sems.at[9])
     out.start()
     phase("o_finish")
@@ -669,8 +685,8 @@
             vm((6, 8, 128, 128), bf16), vm((6, 8, 128, 128), bf16),
             vm((6, 4, 256, 128), bf16), vm((6, 4, 256, 128), bf16),
             vm((2, 512, 128), bf16), vm((3, 2, 128, 128), bf16), vm((2, 128, 128), bf16), vm((3, 64, 128), bf16),
-            vm((2, 8, 128, 128), bf16), vm((3, 8, 64, 128), bf16), vm((8, 64, 128), bf16), vm((7, 64, 128), bf16),
-            vm((8, 256, 128), bf16), vm((3, 8, 64, 128), bf16), vm((8, 64, 128), bf16), vm((7, 64, 128), bf16),
+            vm((2, 8, 128, 128), bf16), vm((2, 3, 4, 64, 128), bf16), vm((8, 64, 128), bf16), vm((8, 64, 128), bf16),
+            vm((8, 256, 128), bf16), vm((2, 3, 4, 64, 128), bf16), vm((8, 64, 128), bf16), vm((8, 64, 128), bf16),
             vm((MATS, KV, 128), bf16), vm((MATS, 32, 128), bf16), vm((8, 8, 128), f32), vm((32, 8, 128), f32),
             vm((MATS, 64, 128), f32), vm((16, 32, 128), bf16), vm((16, 64, 128), bf16), vm((16, 128), f32),
             vm((64, D), bf16), vm((64, D), bf16), vm((KV, D), bf16), vm((KV, D), bf16), vm((32, 32, 128), bf16), vm((MATS, KV, 128), bf16),

time: 101 us -> 98.7 us (0.977)
  Pallas kernels: 100 us -> 98 us
    pallas_call x1, Pallas kernels: 97.3 us -> 95.1 us  [stepped(): pl.pallas_call(step_kernel, out_shape=(jax.ShapeDtypeStruct((MATS, KV, 12...]
where the time goes in v4:
time: 98.7 us
  Pallas kernels  98 us (99%)
    pallas_call x1, Pallas kernels, stepped(): pl.pallas_call(step_kernel, out_shape=(jax.ShapeDtypeStruct((MATS, KV, 12...  95.1 us
    pallas_call x1, Pallas kernels, finished(): pl.pallas_call(finish_kernel, grid=(4,), out_shape=(jax.ShapeDtypeStruct(...  2.88 us

profile of v4, /device:TPU:1, one launch (start us, length us, event | category | flops | bytes accessed | tf_op | source)
XLA Modules:
  0.0 98.7 jit_solution(6208105234804122894)
XLA Ops:
  0.6 0.0 copy-start
  0.6 95.1 %step.1 = (bf16[12,256,128]{2,1,0:T(8,128)(2,1)S(1)}, f32[16,128]{1,0:T(8,128)S(1)}, bf16[12,256,128]{2,1,0:T(8,128)(2,1)S(1)}, bf16[2,256,2048]{2,1,0:T(8,128)(2,1)S(1)}) custom-call(s32[12]{0:T(128)} %owners_in.1, s32[2]{0:T(128)} %starts_in.1, bf16[6,128,2048]{2,1,0:T(8,128)(2,1)} %act.1, bf16[6,128,512]{2,1,0:T(8,128)(2,1)} %cot.1, f32[12,256,128]{2,1,0:T(8,128)} %mom.3), custom_call_target="tpu_custom_call" | custom-call | tf_op jit(solution)/shard_map/step/pallas_call | solution.py:667
  95.8 0.0 copy-done
  95.8 2.9 %finish.1 = (f32[12,256,128]{2,1,0:T(8,128)}, f32[12,256,128]{2,1,0:T(8,128)}, bf16[2,256,2048]{2,1,0:T(8,128)(2,1)}) custom-call(f32[16,128]{1,0:T(8,128)S(1)} %get-tuple-element.7.factors, bf16[12,256,128]{2,1,0:T(8,128)(2,1)S(1)} %get-tuple-element.8.g, f32[12,256,128]{2,1,0:T(8,128)S(1)} %copy-done, bf16[12,256,128]{2,1,0:T(8,128)(2,1)S(1)} %get-tuple-element.9.x, ...), custom_call_target="tpu_custom_call" | custom-call | tf_op jit(solution)/shard_map/finish/pallas_call | solution.py:720
Async XLA Ops:
  0.6 95.1 %copy-start = (f32[12,256,128]{2,1,0:T(8,128)S(1)}, f32[12,256,128]{2,1,0:T(8,128)}, u32[]{:S(2)}) copy-start(f32[12,256,128]{2,1,0:T(8,128)} %mom.3) | copy-start | bytes 4718596

commit v5 on v4

--- a/solution.py
+++ b/solution.py
@@ -159,7 +159,7 @@
 Z_BASE = {(0, 1): 0, (1, -1): 4, (1, 1): 8, (0, -1): 11}
 PAIR_BASE = {(0, 1): 0, (1, -1): 2, (1, 1): 4, (0, -1): 5}
 PAIR_STEPS = {(0, 1): 2, (1, -1): 2, (1, 1): 1, (0, -1): 1}
-OUTLETS, ARRIVALS = 39, 67
+OUTLETS, ARRIVALS = 29, 68
 
 
 def step_kernel(
@@ -183,7 +183,7 @@
         loads_out[j].start()
         loads[j].start()
     rows = rows_at(me.block * 32, 32)
-    load_momentum = pltpu.make_async_copy(mom.at[:, rows_at(x * 64, 64), :], mb, local_sems.at[12])
+    load_momentum = pltpu.make_async_copy(mom.at[:, rows, :], mb, local_sems.at[12])
     load_momentum.start()
     load_owners = pltpu.make_async_copy(owners_in, owners, local_sems.at[10])
     load_starts = pltpu.make_async_copy(starts_in, starts, local_sems.at[11])
@@ -192,8 +192,11 @@
 
     phase("r_greet")
     plane = [(dx, dy, dc) for dx in range(4) for dy in range(4) for dc in range(2) if dx or dy or dc]
-    devices = [me.near(dx, dy, dc, 0) for dx, dy, dc in plane]
-    devices += [me.near(0, dy, 0, dz) for dy in range(4) for dz in range(1, 8)]
+    devices = [me.partner()]
+    devices += [me.near(d, 0, 0, 0) for d in range(1, 4)]
+    devices += [me.near(0, d, 0, 0) for d in range(1, 4)]
+    devices += [me.near(0, 0, 0, d) for d in range(1, 8)]
+    devices += [(x, yh, c, wrap(z + d, 8), 1 - yl) for d in range(1, 8)]
     signal_all(devices)
 
     def turn(source, store, inner_is_x):
@@ -347,7 +350,8 @@
     load_starts.wait()
     lax.fori_loop(0, 16, note, 0)
     gather_columns(mb, ms)
-    mq[:, here] = ms[me.column]
+    own_half = rows_at(yh * 32, 32)
+    mq[own_half, here] = ms[me.column]
 
     phase("r_z2")
     z_round(2, True)
@@ -364,7 +368,7 @@
     z_round(3, False)
     phase("r_z4")
     z_round(4)
-    copies = [(ms.at[p], mq.at[:, here], device) for device, p in me.columns()]
+    copies = [(ms.at[p], mq.at[own_half, here], device) for device, p in me.columns()]
     momentum_to_owner = wire.group(copies, ms.at[:15])
 
     phase("r_xlast")
@@ -432,25 +436,21 @@
             sent["z", half, d, n].wait_recv()
             last.append(Z_BASE[half, d] + n - 1)
         value = z_part(z, half) + zr[last[0]].astype(f32) + zr[last[1]].astype(f32)
-        z2s[half] = value.astype(bf16)
+        z2s[half] = value.astype(bf16).reshape(4, 2, 64, 128)
     copies = []
     for d in (1, 3, 2):
-        to = wrap(x + d, 4)
-        copies.append((z2s.at[:, rows_at(to * 128, 128), :], z2r.at[d - 1], me.at(dx=d)))
+        to = wrap(y + d, 4)
+        copies.append((z2s.at[lax.rem(to, 2), :, lax.div(to, 2)], z2r.at[d - 1], me.at_y(d)))
     sent["z2"] = wire.group(copies, z2r)
     def z_second():
         phase("r_z3b")
         sent["z2"].wait_recv()
-        for t in range(2):
-            value = z2s[t, rows_at(x * 128, 128), :].astype(f32)
+        for to in range(4):
+            value = z2s[yl, to, yh].astype(f32)
             for d in range(3):
-                value += z2r[d, t].astype(f32)
-            z3s[t] = value.astype(bf16)
-        copies = []
-        for d in (2, 1, 3):
-            to = wrap(y + d, 4)
-            source = z3s.at[lax.rem(to, 2), rows_at(lax.div(to, 2) * 64, 64), :]
-            copies.append((source, z3r.at[d - 1], me.at_y(d)))
+                value += z2r[d, to].astype(f32)
+            z3s[to] = value.astype(bf16)
+        copies = [(z3s.at[wrap(x + d, 4)], z3r.at[d - 1], me.at(dx=d)) for d in (2, 1, 3)]
         sent["z3"] = wire.group(copies, z3r)
 
     def x_here(e):
@@ -466,8 +466,9 @@
         phase("r_y3" + "ab"[second])
         sent["y2", second].wait_recv()
         sent["y3", second] = third(second, y3s, y2r, y_here, y3r)
-        if second == 0:
-            z_second()
+    z_second()
+    momentum_to_owner.wait_recv()
+    momentum_over = wire.send(mq.at[own_half], mq.at[own_half], me.near(0, 2, 0, 0))
 
     phase("r_xfin")
     inverse = 1.0 / math.sqrt(TOKENS)
@@ -497,7 +498,7 @@
     piece(2, value)
     phase("r_zfin")
     sent["z3"].wait_recv()
-    value = z3s[yl, rows_at(yh * 64, 64), :].astype(f32)
+    value = z3s[x].astype(f32)
     for d in range(3):
         value += z3r[d].astype(f32)
     piece(0, value)
@@ -508,14 +509,13 @@
     swap = wire.send(gp.at[own], gp.at[own], me.partner())
     swap.wait_recv()
     gather_columns(gp, us)
-    half = rows_at(yh * 32, 32)
-    gq[half, here] = us[me.column]
+    gq[own_half, here] = us[me.column]
     copies = []
     for dz in (4, 3, 5, 2, 6, 1, 7, 0):
         for dy in (2, 1, 3, 0):
             if dz or dy:
                 device = me.near(0, dy, 0, dz)
-                copies.append((us.at[2 * device[3] + device[4]], gq.at[half, here], device))
+                copies.append((us.at[2 * device[3] + device[4]], gq.at[own_half, here], device))
     to_owner = wire.group(copies, rb.at[:31])
     phase("r_sqw1b")
     squares.wait_recv()
@@ -529,7 +529,7 @@
     totals = [sum((sq2[k * 16 + i] for i in range(1, 16)), sq2[k * 16]) for k in range(2)]
     totals = jnp.concatenate(totals, axis=0)
     phase("o_a2a")
-    momentum_to_owner.wait_recv()
+    momentum_over.wait_recv()
     to_owner.wait_recv()
     phase("o_choose")
 
@@ -560,14 +560,15 @@
         return gin.at[rows_at(wrap(x + dx, 4) * 64 + 32 * h, 32), :]
 
     ahead, behind = me.at(dx=1), me.at(dx=-1)
-    first_up = wire.send(part(0, 0), part(0, 0), ahead)
-    first_down = wire.send(part(0, 1), part(0, 1), behind)
-    second_up = wire.send(part(0, 1), part(0, 1), ahead)
-    second_down = wire.send(part(0, 0), part(0, 0), behind)
+    out_u = wire.outlet(gin.at[:192])
+    first_up = wire.send(part(0, 0), part(0, 0), ahead, out_u)
+    first_down = wire.send(part(0, 1), part(0, 1), behind, out_u)
+    second_up = wire.send(part(0, 1), part(0, 1), ahead, out_u)
+    second_down = wire.send(part(0, 0), part(0, 0), behind, out_u)
     first_up.wait_recv()
-    third_up = wire.send(part(-1, 0), part(-1, 0), ahead)
+    third_up = wire.send(part(-1, 0), part(-1, 0), ahead, out_u)
     first_down.wait_recv()
-    third_down = wire.send(part(1, 1), part(1, 1), behind)
+    third_down = wire.send(part(1, 1), part(1, 1), behind, out_u)
     for copy in (second_up, second_down, third_up, third_down):
         copy.wait_recv()
     pieces = wire.group(
@@ -601,7 +602,8 @@
             slot = slot + (owners[j] == owner).astype(jnp.int32) * (j < m).astype(jnp.int32)
         ob[m, rows, :] = rb[jnp.minimum(slot, 1) * 16 + owner]
     phase("o_ag2")
-    gathered = [wire.send(ob.at[own, rows, :], ob.at[own, rows, :], device) for device in me.replicas()]
+    out_pieces = wire.outlet(ob.at[:6, :224])
+    gathered = [wire.send(ob.at[own, rows, :], ob.at[own, rows, :], device, out_pieces) for device in me.replicas()]
     onward = wire.opened(ob.at[:6])
     wire.join(onward, [(ob.at[own, rows, :], ob.at[own, rows, :], me.partner())])
     over_g.wait_recv()
@@ -684,11 +686,11 @@
             vm((14, 512, 128), bf16), vm((14, 512, 128), bf16),
             vm((6, 8, 128, 128), bf16), vm((6, 8, 128, 128), bf16),
             vm((6, 4, 256, 128), bf16), vm((6, 4, 256, 128), bf16),
-            vm((2, 512, 128), bf16), vm((3, 2, 128, 128), bf16), vm((2, 128, 128), bf16), vm((3, 64, 128), bf16),
+            vm((2, 4, 2, 64, 128), bf16), vm((3, 4, 64, 128), bf16), vm((4, 64, 128), bf16), vm((3, 64, 128), bf16),
             vm((2, 8, 128, 128), bf16), vm((2, 3, 4, 64, 128), bf16), vm((8, 64, 128), bf16), vm((8, 64, 128), bf16),
             vm((8, 256, 128), bf16), vm((2, 3, 4, 64, 128), bf16), vm((8, 64, 128), bf16), vm((8, 64, 128), bf16),
             vm((MATS, KV, 128), bf16), vm((MATS, 32, 128), bf16), vm((8, 8, 128), f32), vm((32, 8, 128), f32),
-            vm((MATS, 64, 128), f32), vm((16, 32, 128), bf16), vm((16, 64, 128), bf16), vm((16, 128), f32),
+            vm((MATS, 32, 128), f32), vm((16, 32, 128), bf16), vm((16, 32, 128), bf16), vm((16, 128), f32),
             vm((64, D), bf16), vm((64, D), bf16), vm((KV, D), bf16), vm((KV, D), bf16), vm((32, 32, 128), bf16), vm((MATS, KV, 128), bf16),
             vm((KV, KV), f32),
             pltpu.SMEM((MATS,), jnp.int32), pltpu.SMEM((2,), jnp.int32), pltpu.SMEM((2, 16), jnp.int32),
@@ -703,30 +705,45 @@
     )(*operands)
 
 
-def finish_kernel(factors, g, mom, x, whole, mom_out, update, owned):
-    i = pl.program_id(0)
+def finish_kernel(factors, g, mom, x, whole, mom_out, update, owned, mv, uv, ov, sems):
     scale = math.sqrt(max(KV, D))
-    for k in range(3):
-        m = 3 * i + k
-        factor = factors[pl.ds(m + 2 * (m >= 6).astype(jnp.int32), 1), :]
-        mom_out[k] = momentum_rate * mom[k] + factor * g[k].astype(f32)
-    update[...] = scale * x[...].astype(f32)
-    owned[...] = (scale * whole[...].astype(f32)).astype(bf16)
+    copies = []
+
+    def store(source, target):
+        copy = pltpu.make_async_copy(source, target, sems.at[len(copies)])
+        copy.start()
+        copies.append(copy)
+
+    for i in range(4):
+        rows, mats = pl.ds(64 * i, 64), pl.ds(3 * i, 3)
+        ov[:, rows] = (scale * whole[:, rows].astype(f32)).astype(bf16)
+        store(ov.at[:, rows], owned.at[:, rows])
+        for m in range(3 * i, 3 * i + 3):
+            r = m if m < 6 else m + 2
+            mv[m] = momentum_rate * mom[m] + factors[r : r + 1, :] * g[m].astype(f32)
+        store(mv.at[mats], mom_out.at[mats])
+        uv[mats] = scale * x[mats].astype(f32)
+        store(uv.at[mats], update.at[mats])
+    for copy in copies:
+        copy.wait()
 
 
 def finished(factors, g, mom, x, whole):
-    part = pl.BlockSpec((3, KV, 128), lambda i: (i, 0, 0))
-    rows = pl.BlockSpec((2, KV // 4, D), lambda i: (0, i, 0))
     return pl.pallas_call(
         finish_kernel,
-        grid=(4,),
         out_shape=(
             jax.ShapeDtypeStruct((MATS, KV, 128), f32),
             jax.ShapeDtypeStruct((MATS, KV, 128), f32),
             jax.ShapeDtypeStruct((2, KV, D), bf16),
         ),
-        in_specs=[pl.BlockSpec((16, 128), lambda i: (0, 0)), part, part, part, rows],
-        out_specs=(part, part, rows),
+        in_specs=[pl.BlockSpec(memory_space=pltpu.VMEM)] * 5,
+        out_specs=[pl.BlockSpec(memory_space=pltpu.HBM)] * 3,
+        scratch_shapes=[
+            pltpu.VMEM((MATS, KV, 128), f32),
+            pltpu.VMEM((MATS, KV, 128), f32),
+            pltpu.VMEM((2, KV, D), bf16),
+            pltpu.SemaphoreType.DMA((12,)),
+        ],
         compiler_params=pltpu.CompilerParams(vmem_limit_bytes=16 * 1024 * 1024),
         name="finish",
     )(factors, g, mom, x, whole)

time: 98.7 us -> 96.7 us (0.980)
  Pallas kernels: 98 us -> 96 us
    pallas_call x1, Pallas kernels: 95.1 us -> 93.5 us  [stepped(): pl.pallas_call(step_kernel, out_shape=(jax.ShapeDtypeStruct((MATS, KV, 12...]
where the time goes in v5:
time: 96.7 us; the launch traced here: 96.6 us
  Pallas kernels  96 us (99%)
    pallas_call x1, Pallas kernels, stepped(): pl.pallas_call(step_kernel, out_shape=(jax.ShapeDtypeStruct((MATS, KV, 12...  93.5 us
    pallas_call x1, Pallas kernels, finished(): pl.pallas_call(finish_kernel, out_shape=(jax.ShapeDtypeStruct((MATS, KV,...  2.52 us

profile of v5, /device:TPU:1, one launch (start us, length us, event | category | flops | bytes accessed | tf_op | source)
XLA Modules:
  0.0 96.6 jit_solution(3358410707110961441)
XLA Ops:
  0.6 0.0 copy-start
  0.6 93.5 %step.1 = (bf16[12,256,128]{2,1,0:T(8,128)(2,1)S(1)}, f32[16,128]{1,0:T(8,128)S(1)}, bf16[12,256,128]{2,1,0:T(8,128)(2,1)S(1)}, bf16[2,256,2048]{2,1,0:T(8,128)(2,1)S(1)}) custom-call(s32[12]{0:T(128)} %owners_in.1, s32[2]{0:T(128)} %starts_in.1, bf16[6,128,2048]{2,1,0:T(8,128)(2,1)} %act.1, bf16[6,128,512]{2,1,0:T(8,128)(2,1)} %cot.1, f32[12,256,128]{2,1,0:T(8,128)} %mom.3), custom_call_target="tpu_custom_call" | custom-call | tf_op jit(solution)/shard_map/step/pallas_call | solution.py:669
  94.1 0.0 copy-done
  94.1 2.5 %finish.1 = (f32[12,256,128]{2,1,0:T(8,128)}, f32[12,256,128]{2,1,0:T(8,128)}, bf16[2,256,2048]{2,1,0:T(8,128)(2,1)}) custom-call(f32[16,128]{1,0:T(8,128)S(1)} %get-tuple-element.7.factors, bf16[12,256,128]{2,1,0:T(8,128)(2,1)S(1)} %get-tuple-element.8.g, f32[12,256,128]{2,1,0:T(8,128)S(1)} %copy-done, bf16[12,256,128]{2,1,0:T(8,128)(2,1)S(1)} %get-tuple-element.9.x, ...), custom_call_target="tpu_custom_call" | custom-call | tf_op jit(solution)/shard_map/finish/pallas_call | solution.py:732
Async XLA Ops:
  0.6 93.5 %copy-start = (f32[12,256,128]{2,1,0:T(8,128)S(1)}, f32[12,256,128]{2,1,0:T(8,128)}, u32[]{:S(2)}) copy-start(f32[12,256,128]{2,1,0:T(8,128)} %mom.3) | copy-start | bytes 4718596

commit v6 on v5

--- a/solution.py
+++ b/solution.py
@@ -64,7 +64,7 @@
             yield (wrap(self.x + dx, 4), lax.rem(self.yh + dyh, 2), self.c, self.z, self.yl)
 
     def offsets(self):
-        return ((1, 0), (3, 0), (0, 1), (2, 0), (1, 1), (3, 1), (2, 1))
+        return ((2, 1), (1, 1), (3, 1), (2, 0), (0, 1), (1, 0), (3, 0))
 
     def columns_at(self, dz):
         for dyl in range(2):
@@ -208,9 +208,7 @@
                     to = (by * 256 + bx * 64 if inner_is_x else bx * 128 + by * 64) + kv * 32
                     store(to, turned[at : at + 32, :])
 
-    load_cot.wait()
-    for j in (1, 2, 0):
-
+    def turn_layer(j):
         def store_out(to, value, j=j):
             cout[j, to : to + 32, :] = value
 
@@ -220,6 +218,8 @@
         turn(cin[3 * (1 - c) + j], store_out, j == 2)
         turn(cin[3 * c + j], store_own, j == 2)
 
+    load_cot.wait()
+    turn_layer(1)
     phase("r_greetw")
     pl.semaphore_wait(pltpu.get_barrier_semaphore(), len(devices))
     phase("r_swap")
@@ -227,6 +227,8 @@
     out_x, out_y, out_z = wire.outlet(xs), wire.outlet(ys), wire.outlet(zs)
     swaps = {}
     for j in (1, 2, 0):
+        if j != 1:
+            turn_layer(j)
         loads_out[j].wait()
         swaps[j] = [wire.send(cout.at[j], cott.at[j, :, mine], me.partner(), out_cot)]
         parts = 2 if j == 1 else 1
@@ -402,7 +404,7 @@
         lax.fori_loop(0, 4, x_last, 0, unroll=True)
     for second in range(2):
         copies = []
-        for d in (1, 3, 2):
+        for d in (2, 1, 3):
             to = wrap(y + d, 4)
             source = x2s.at[lax.rem(to, 2), pl.ds(4 * second, 4), rows_at(lax.div(to, 2) * 64, 64), :]
             copies.append((source, x2r.at[second, d - 1], me.at_y(d)))
@@ -423,7 +425,7 @@
         lax.fori_loop(0, 4, y_last, 0, unroll=True)
     for second in range(2):
         copies = []
-        for d in (1, 3, 2):
+        for d in (2, 1, 3):
             source = y2s.at[pl.ds(4 * second, 4), rows_at(wrap(x + d, 4) * 64, 64), :]
             copies.append((source, y2r.at[second, d - 1], me.at(dx=d)))
         sent["y2", second] = wire.group(copies, y2r.at[second])
@@ -520,9 +522,10 @@
     phase("r_sqw1b")
     squares.wait_recv()
     spot = c * 16 + 4 * x + y
+    farthest = sorted(plane, key=lambda d: -min(d[0], 4 - d[0]) - min(d[1], 4 - d[1]))
     sq2[spot] = sum((sqs[i] for i in range(1, 8)), sqs[0])
     squares = wire.group(
-        [(sq2.at[spot], sq2.at[spot], me.near(dx, dy, dc, 0)) for dx, dy, dc in plane], sq2.at[:31]
+        [(sq2.at[spot], sq2.at[spot], me.near(dx, dy, dc, 0)) for dx, dy, dc in farthest], sq2.at[:31]
     )
     phase("r_sqw2")
     squares.wait_recv()

time: 96.7 us -> 95.4 us (0.987)
  Pallas kernels: 96 us -> 94.7 us
    pallas_call x1, Pallas kernels: 93.5 us -> 92.1 us  [stepped(): pl.pallas_call(step_kernel, out_shape=(jax.ShapeDtypeStruct((MATS, KV, 12...]
where the time goes in v6:
time: 95.4 us; the launch traced here: 95.3 us
  Pallas kernels  94.7 us (99%)
    pallas_call x1, Pallas kernels, stepped(): pl.pallas_call(step_kernel, out_shape=(jax.ShapeDtypeStruct((MATS, KV, 12...  92.1 us
    pallas_call x1, Pallas kernels, finished(): pl.pallas_call(finish_kernel, out_shape=(jax.ShapeDtypeStruct((MATS, KV,...  2.52 us

profile of v6, /device:TPU:1, one launch (start us, length us, event | category | flops | bytes accessed | tf_op | source)
XLA Modules:
  0.0 95.3 jit_solution(9684407083236700648)
XLA Ops:
  0.6 0.0 copy-start
  0.6 92.1 %step.1 = (bf16[12,256,128]{2,1,0:T(8,128)(2,1)S(1)}, f32[16,128]{1,0:T(8,128)S(1)}, bf16[12,256,128]{2,1,0:T(8,128)(2,1)S(1)}, bf16[2,256,2048]{2,1,0:T(8,128)(2,1)S(1)}) custom-call(s32[12]{0:T(128)} %owners_in.1, s32[2]{0:T(128)} %starts_in.1, bf16[6,128,2048]{2,1,0:T(8,128)(2,1)} %act.1, bf16[6,128,512]{2,1,0:T(8,128)(2,1)} %cot.1, f32[12,256,128]{2,1,0:T(8,128)} %mom.3), custom_call_target="tpu_custom_call" | custom-call | tf_op jit(solution)/shard_map/step/pallas_call | solution.py:672
  92.8 0.0 copy-done
  92.8 2.5 %finish.1 = (f32[12,256,128]{2,1,0:T(8,128)}, f32[12,256,128]{2,1,0:T(8,128)}, bf16[2,256,2048]{2,1,0:T(8,128)(2,1)}) custom-call(f32[16,128]{1,0:T(8,128)S(1)} %get-tuple-element.7.factors, bf16[12,256,128]{2,1,0:T(8,128)(2,1)S(1)} %get-tuple-element.8.g, f32[12,256,128]{2,1,0:T(8,128)S(1)} %copy-done, bf16[12,256,128]{2,1,0:T(8,128)(2,1)S(1)} %get-tuple-element.9.x, ...), custom_call_target="tpu_custom_call" | custom-call | tf_op jit(solution)/shard_map/finish/pallas_call | solution.py:735
Async XLA Ops:
  0.6 92.2 %copy-start = (f32[12,256,128]{2,1,0:T(8,128)S(1)}, f32[12,256,128]{2,1,0:T(8,128)}, u32[]{:S(2)}) copy-start(f32[12,256,128]{2,1,0:T(8,128)} %mom.3) | copy-start | bytes 4718596

commit v7 on v6

--- a/solution.py
+++ b/solution.py
@@ -159,7 +159,7 @@
 Z_BASE = {(0, 1): 0, (1, -1): 4, (1, 1): 8, (0, -1): 11}
 PAIR_BASE = {(0, 1): 0, (1, -1): 2, (1, 1): 4, (0, -1): 5}
 PAIR_STEPS = {(0, 1): 2, (1, -1): 2, (1, 1): 1, (0, -1): 1}
-OUTLETS, ARRIVALS = 29, 68
+OUTLETS, ARRIVALS = 29, 69
 
 
 def step_kernel(
@@ -231,7 +231,7 @@
             turn_layer(j)
         loads_out[j].wait()
         swaps[j] = [wire.send(cout.at[j], cott.at[j, :, mine], me.partner(), out_cot)]
-        parts = 2 if j == 1 else 1
+        parts = 2 if j else 1
         for k in range(parts):
             cols = pl.ds(k * (D // parts), D // parts)
             swaps[j].append(
@@ -315,6 +315,7 @@
     phase("r_y1")
     prepare(2)
     y_send(0, 1, 1)
+    swaps[2][2].wait_recv()
     y_send(1, -1, 1)
     phase("r_z1")
     prepare(0)

time: 95.4 us -> 95.3 us (level)
  no operation moved by 1% of the time
where the time goes in v7:
time: 95.3 us
  Pallas kernels  94.6 us (99%)
    pallas_call x1, Pallas kernels, stepped(): pl.pallas_call(step_kernel, out_shape=(jax.ShapeDtypeStruct((MATS, KV, 12...  92.1 us
    pallas_call x1, Pallas kernels, finished(): pl.pallas_call(finish_kernel, out_shape=(jax.ShapeDtypeStruct((MATS, KV,...  2.52 us

profile of v7, /device:TPU:1, one launch (start us, length us, event | category | flops | bytes accessed | tf_op | source)
XLA Modules:
  0.0 95.3 jit_solution(9502100958103152080)
XLA Ops:
  0.6 0.0 copy-start
  0.6 92.1 %step.1 = (bf16[12,256,128]{2,1,0:T(8,128)(2,1)S(1)}, f32[16,128]{1,0:T(8,128)S(1)}, bf16[12,256,128]{2,1,0:T(8,128)(2,1)S(1)}, bf16[2,256,2048]{2,1,0:T(8,128)(2,1)S(1)}) custom-call(s32[12]{0:T(128)} %owners_in.1, s32[2]{0:T(128)} %starts_in.1, bf16[6,128,2048]{2,1,0:T(8,128)(2,1)} %act.1, bf16[6,128,512]{2,1,0:T(8,128)(2,1)} %cot.1, f32[12,256,128]{2,1,0:T(8,128)} %mom.3), custom_call_target="tpu_custom_call" | custom-call | tf_op jit(solution)/shard_map/step/pallas_call | solution.py:673
  92.7 0.0 copy-done
  92.7 2.5 %finish.1 = (f32[12,256,128]{2,1,0:T(8,128)}, f32[12,256,128]{2,1,0:T(8,128)}, bf16[2,256,2048]{2,1,0:T(8,128)(2,1)}) custom-call(f32[16,128]{1,0:T(8,128)S(1)} %get-tuple-element.7.factors, bf16[12,256,128]{2,1,0:T(8,128)(2,1)S(1)} %get-tuple-element.8.g, f32[12,256,128]{2,1,0:T(8,128)S(1)} %copy-done, bf16[12,256,128]{2,1,0:T(8,128)(2,1)S(1)} %get-tuple-element.9.x, ...), custom_call_target="tpu_custom_call" | custom-call | tf_op jit(solution)/shard_map/finish/pallas_call | solution.py:736
Async XLA Ops:
  0.6 92.1 %copy-start = (f32[12,256,128]{2,1,0:T(8,128)S(1)}, f32[12,256,128]{2,1,0:T(8,128)}, u32[]{:S(2)}) copy-start(f32[12,256,128]{2,1,0:T(8,128)} %mom.3) | copy-start | bytes 4718596
